TPU v7x, 256 devices: a whole 4x4x8 slice. The times are simulated.
256 devices in a mesh: row: 8 (over y, x_lo), col: 32 (over z, x_hi, core).
Axes of the slice: x: 4 (x_hi: 2, x_lo: 2; x = x_hi * 2 + x_lo), y: 4, z: 8, core: 2. Of those that a mesh axis runs over, the one named last changes fastest.
Arguments:
- density: bfloat16 [8192, 8192], P('row', 'col'), may hold values from -0.0625 to 0.0625
- density_mask: int32 [64, 64], P('row', 'col'), may hold values from 0 to 1, as said below
- response: bfloat16 [2, 8192, 8192], P(None, 'row', 'col'), may hold values from -6 to 6
- response_mask: int32 [2, 64, 64], P(None, 'row', 'col'), may hold values from 0 to 1, as said below
- filter_mask: int32 [64, 64], P('row', 'col'), may hold values from 0 to 1, as said below
Outputs:
- product: bfloat16 [2, 8192, 8192], P(None, 'row', 'col')
Inputs may be any that keep to these rules, and one draw needn't show every extreme that they name: `density_mask`: diagonal blocks are always nonzero; blocks within cyclic block distance 8 of the diagonal are more often nonzero than blocks further out; whole block rows and whole block columns may be nonzero. `response_mask`: for each direction, diagonal blocks are always nonzero; blocks within cyclic block distance 8 of the diagonal are more often nonzero than blocks further out; whole block rows and whole block columns may be nonzero. `filter_mask`: diagonal blocks are always kept; blocks within cyclic block distance 2 * 8 of the diagonal are more often kept than blocks further out; whole block rows and whole block columns may be kept.
All inputs are finite; a program needn't handle non-finite values.
Results may differ from a plain program's by a relative error of at most 0.001.
Values may be sent and summed in bfloat16 or wider, within the bound.
No kernel may reach another device: no remote copies, remote signals or barrier semaphores. Data moves between devices by JAX's collectives and lax.ppermute only.
A program may use at most 128 MiB of HBM per device.

v0:
```python
import jax
import jax.numpy as jnp
from jax import lax
from jax.sharding import PartitionSpec as P


def in_order(tiles, dim):
    dims = list(tiles.shape[1:])
    dims[dim] *= tiles.shape[0]
    return jnp.moveaxis(tiles, 0, dim).reshape(dims)


def sent_to_all(array, axis):
    peers = lax.axis_size(axis)
    return lax.all_to_all(
        jnp.broadcast_to(array[None], (peers, *array.shape)), axis, 0, 0, tiled=True
    )


def gather_directly(array, axis, dim):
    return in_order(sent_to_all(array, axis), dim)


def expand_blocks(values, mask, blocksize):
    lead = values.shape[:-2]
    height = values.shape[-2] // blocksize
    width = values.shape[-1] // blocksize
    shaped = values.reshape(lead + (height, blocksize, width, blocksize))
    scaled = shaped * mask.astype(values.dtype)[..., :, None, :, None]
    return scaled.reshape(values.shape)


def body(density, density_mask, response, response_mask, filter_mask):
    blocksize = density.shape[1] // density_mask.shape[1]
    masked_density = expand_blocks(density, density_mask, blocksize)
    masked_response = expand_blocks(response, response_mask, blocksize)
    density_full = lax.all_gather(masked_density, "col", axis=1, tiled=True)
    result = jnp.einsum(
        "ik,dkj->dij",
        density_full,
        gather_directly(masked_response, "row", 1),
        preferred_element_type=jnp.float32,
    )
    return expand_blocks(result, filter_mask, blocksize).astype(jnp.bfloat16)


def solution(mesh):
    in_specs = (
        P("row", "col"),
        P("row", "col"),
        P(None, "row", "col"),
        P(None, "row", "col"),
        P("row", "col"),
    )
    out_specs = P(None, "row", "col")
    return jax.shard_map(body, mesh=mesh, in_specs=in_specs, out_specs=out_specs, check_vma=False)
```

profile of v0, /device:TPU:1, one launch (start us, length us, event | category | flops | bytes accessed | tf_op | source)
XLA Modules:
  0.0 235.9 jit_solution(5093998022321355920)
XLA Ops:
  6.5 0.0 all-gather.2.cloned.1.call-start
  6.5 0.7 convert_element_type.13
  7.2 0.1 copy.13
  7.3 0.3 mul.39
  7.7 1.9 bitcast_multiply_fusion.1
  9.6 0.0 all-gather.2.cloned.1.call-update
  9.6 0.7 convert_element_type.12
  10.3 0.1 copy.10
  10.4 0.6 mul.36
  11.0 0.7 mul.37
  11.7 1.5 mul.38
  13.2 0.5 copy.11
  13.8 4.3 %broadcast_in_dim.2 = bf16[8,2,1024,256]{2,3,1,0:T(8,128)(2,1)} broadcast(bf16[2,1024,256]{1,2,0:T(8,128)(2,1)S(1)} %copy.11), dimensions={1,2,3} | broadcast | bytes 9437184 | tf_op jit(solution)/shard_map/broadcast_in_dim | solution.py:16
  18.1 0.0 copy-start
  18.1 6.1 %all-to-all-start = ((bf16[8,2,1024,256]{2,3,1,0:T(8,128)(2,1)}), bf16[8,2,1024,256]{2,3,1,0:T(8,128)(2,1)}, u32[]{:S(2)}, u32[]{:S(2)}) async-start(bf16[8,2,1024,256]{2,3,1,0:T(8,128)(2,1)} %broadcast_in_dim.2), calls=%async_computation | async-start | bytes 16777216 | tf_op jit(solution)/shard_map/all_to_all | solution.py:15
  24.1 0.0 copy-done
  24.1 0.1 mul.42
  24.3 0.2 copy.20
  24.5 136.0 %all-to-all-done = bf16[8,2,1024,256]{2,3,1,0:T(8,128)(2,1)} async-done(((bf16[8,2,1024,256]{2,3,1,0:T(8,128)(2,1)}), bf16[8,2,1024,256]{2,3,1,0:T(8,128)(2,1)}, u32[]{:S(2)}, u32[]{:S(2)}) %all-to-all-start) | async-done | bytes 8388640 | tf_op jit(solution)/shard_map/all_to_all | solution.py:15
  160.5 8.0 %copy.15 = bf16[8,2,32,8,1024]{4,3,0,2,1:T(8,128)(2,1)} copy(bf16[8,2,32,8,1024]{4,3,2,1,0:T(8,128)(2,1)} %bitcast.3) | data formatting | bytes 16777216 | tf_op jit(solution)/shard_map/reshape | solution.py:10
  168.6 44.4 %all-gather.2.cloned.1.call-done = bf16[1024,8192]{1,0:T(8,128)(2,1)} async-done(((bf16[1024,256]{1,0:T(8,128)(2,1)}), bf16[1024,8192]{1,0:T(8,128)(2,1)}) %all-gather.2.cloned.1.call-update) | async-done | bytes 16777232 | tf_op jit(solution)/shard_map/all_gather | solution.py:37
  212.9 14.8 %fusion.2 = bf16[2,1024,256]{1,2,0:T(8,128)(2,1)S(1)} fusion(bf16[2,8192,256]{1,2,0:T(8,128)(2,1)} %bitcast.24, bf16[1024,8192]{1,0:T(8,128)(2,1)} %all-gather.2.cloned.1.call-done, f32[1024,256]{0,1:T(8,128)S(1)} %bitcast.27), kind=kOutput, calls=%fused_computation.3 | convolution fusion | flops 8590983168 | bytes 27262976 | tf_op jit(solution)/shard_map/ik,dkj->dij/dot_general | solution.py:38
  227.8 1.3 copy.14
  (1 shorter events, 0.0 us)
Async XLA Ops:
  6.5 206.4 %all-gather.2.cloned.1.call-start = ((), (), s32[]{:S(2)}) async-start(), calls=%async_computation.1 | async-start | bytes 17301504 | tf_op jit(solution)/shard_map/all_gather | solution.py:37
  18.1 6.1 %copy-start = (s32[8,2]{0,1:T(2,128)S(1)}, s32[8,2]{0,1:T(2,128)}, u32[]{:S(2)}) copy-start(s32[8,2]{0,1:T(2,128)} %param.9) | copy-start | bytes 196
  18.1 142.5 %all-to-all-start = ((bf16[8,2,1024,256]{2,3,1,0:T(8,128)(2,1)}), bf16[8,2,1024,256]{2,3,1,0:T(8,128)(2,1)}, u32[]{:S(2)}, u32[]{:S(2)}) async-start(bf16[8,2,1024,256]{2,3,1,0:T(8,128)(2,1)} %broadcast_in_dim.2), calls=%async_computation | async-start | bytes 16777216 | tf_op jit(solution)/shard_map/all_to_all | solution.py:15
Sparse Core Ops, SparseCore 0:
  9.9 202.9 all-gather.1
where the time goes:
time: 236 us
  waiting for transfers between devices  180 us (76%)
  local copies, waits for them, and re-layouts  16.4 us (7%)
  matrix products  14.8 us (6%)
  between operations  13.5 us (6%)
  starting transfers between devices  6.07 us (3%)
  other arithmetic  4.77 us (2%)
    all_to_all x1, waiting for transfers between devices, sent_to_all(): lax.all_to_all(jnp.broadcast_to(array[None], (peers, *array.shape)), axis...  136 us
    all_gather x1, waiting for transfers between devices, body(): density_full = lax.all_gather(masked_density, 'col', axis=1, tiled=True)  44.4 us
    dot_general x1, matrix products, body(): jnp.einsum('ik,dkj->dij', density_full, gather_directly(masked_response,...  14.8 us
    reshape x1, local copies, waits for them, and re-layouts, in_order(): return jnp.moveaxis(tiles, 0, dim).reshape(dims)  8.04 us
    all_to_all x1, starting transfers between devices, sent_to_all(): lax.all_to_all(jnp.broadcast_to(array[None], (peers, *array.shape)), axis...  6.07 us
  transfers between devices with their start and end apart: 2, of which 2 were waited for; matrix products, arithmetic and copies ran while one was open for 7% of the time, Pallas kernels for 0%

commit v1 on v0

v1 whole, which is shorter than its diff:
```python
import functools

import jax
import jax.numpy as jnp
from jax import lax
from jax.experimental import pallas as pl
from jax.experimental.pallas import tpu as pltpu
from jax.sharding import PartitionSpec as P


BLOCK = 128
ROWS = 1024
COLS = 256
UNIT = 512
VMEM_LIMIT = 60 * 2**20
AHEAD = 3
NZ, NY = 8, 4


def col_pairs(step):
    pairs = []
    for c in range(32):
        z, hi, core = step(c // 4, (c // 2) % 2, c % 2)
        pairs.append((c, (z % NZ) * 4 + (hi % 2) * 2 + core % 2))
    return pairs


def along_z(v):
    return lax.ppermute(v, "col", col_pairs(lambda z, hi, core: (z + 1 - 2 * core, hi, core)))


def across_x(v):
    return lax.ppermute(v, "col", col_pairs(lambda z, hi, core: (z, hi + 1, core)))


def other_core(v):
    return lax.ppermute(v, "col", col_pairs(lambda z, hi, core: (z, hi, core + 1)))


def along_y(v):
    pairs = []
    for r in range(8):
        for c in range(32):
            y = (r // 2 + 1 - 2 * (c % 2)) % NY
            pairs.append((r * 32 + c, (y * 2 + r % 2) * 32 + c))
    return lax.ppermute(v, ("row", "col"), pairs)


def beside_x(v):
    return lax.ppermute(v, "row", [(r, r ^ 1) for r in range(8)])


def mask_kernel(mask, values, out, *apart):
    for i in range(8):
        for j in range(2):
            at = (slice(i * BLOCK, (i + 1) * BLOCK), slice(j * BLOCK, (j + 1) * BLOCK))
            if not apart:
                out[at] = values[at] * mask[j, i].astype(jnp.bfloat16)
            for d, copy in enumerate(apart):
                block = values[(d, *at)] * mask[d, j, i].astype(jnp.bfloat16)
                out[(d, *at)] = block
                copy[at] = block


def masked(values, mask):
    out = [jax.ShapeDtypeStruct(values.shape, values.dtype)]
    if len(values.shape) == 3:
        out += [jax.ShapeDtypeStruct(values.shape[1:], values.dtype)] * values.shape[0]
    return pl.pallas_call(
        mask_kernel,
        out_shape=out,
        in_specs=[
            pl.BlockSpec(memory_space=pltpu.SMEM),
            pl.BlockSpec(memory_space=pltpu.VMEM),
        ],
        out_specs=[pl.BlockSpec(memory_space=pltpu.VMEM)] * len(out),
        cost_estimate=pl.CostEstimate(flops=10**6, bytes_accessed=2**20, transcendentals=0),
    )(jnp.swapaxes(mask, -1, -2), values)


def matmul_kernel(n_a, parts, n_b, pieces, place, keep, *refs):
    a_refs, refs = refs[:n_a], refs[n_a:]
    b_refs, refs = refs[:n_b], refs[n_b:]
    out, a_vm, b_vm, acc, a_sem, b_sem = refs
    row, col = place[0], place[1]
    y, lo = row // 2, row % 2
    z, hi, core = col // 4, (col // 2) % 2, col % 2
    way = 1 - 2 * core
    n_units = len(parts)

    def start(u):
        delta, far = u // 2, u % 2
        head = 1 - core if 1 <= delta <= 3 else core
        for j, (which, index) in enumerate(parts[u]):
            ref = a_refs[which] if index is None else a_refs[which].at[index]
            to = a_vm.at[u, (head + j) % 2]
            pltpu.make_async_copy(ref, to, a_sem.at[u]).start()
        owner = (z + delta * way + NZ) % NZ
        hops = ((y - owner // 2) * way + NY) % NY
        side = (owner % 2 + lo) % 2
        rows = pl.ds(pl.multiple_of(((hi + far) % 2) * UNIT, UNIT), UNIT)
        for i in range(4):
            for low in range(2):

                @pl.when(jnp.logical_and(hops == i, side == low))
                def _():
                    for which, d, at, where in pieces:
                        if (at, where) == (i, low):
                            if d is None:
                                source, target = b_refs[which].at[:, rows, :], b_vm.at[u]
                            else:
                                source, target = b_refs[which].at[rows, :], b_vm.at[u, d]
                            pltpu.make_async_copy(source, target, b_sem.at[u]).start()

    def wait(u):
        pltpu.make_async_copy(b_vm.at[u], b_vm.at[u], b_sem.at[u]).wait()
        pltpu.make_async_copy(a_vm.at[u], a_vm.at[u], a_sem.at[u]).wait()

    for u in range(AHEAD):
        start(u)
    for u in range(n_units):
        if u + AHEAD < n_units:
            start(u + AHEAD)
        wait(u)
        for d in range(2):
            part = sum(
                jnp.dot(
                    a_vm[u, c],
                    b_vm[u, d, c * COLS : (c + 1) * COLS, :],
                    preferred_element_type=jnp.float32,
                )
                for c in range(2)
            )
            if u == 0:
                acc[d] = part
            elif u < n_units - 1:
                acc[d] += part
            else:
                total = acc[d] + part
                for i in range(8):
                    for j in range(2):
                        scale = keep[j, i].astype(jnp.float32)
                        at = (slice(i * BLOCK, (i + 1) * BLOCK), slice(j * BLOCK, (j + 1) * BLOCK))
                        out[(d, *at)] = (total[at] * scale).astype(jnp.bfloat16)


def listed(arrays, array):
    for n, other in enumerate(arrays):
        if other is array:
            return n
    arrays.append(array)
    return len(arrays) - 1


def multiply(place, keep, units, b_parts):
    a_arrays, b_arrays = [], []
    parts = [[(listed(a_arrays, v), index) for v, index in unit] for unit in units]
    pieces = [(listed(b_arrays, v), d, hops, low) for v, d, hops, low in b_parts]
    n_a, n_b = len(a_arrays), len(b_arrays)
    anywhere = pl.BlockSpec(memory_space=pl.ANY)
    scalars = pl.BlockSpec(memory_space=pltpu.SMEM)
    return pl.pallas_call(
        functools.partial(matmul_kernel, n_a, parts, n_b, pieces),
        out_shape=jax.ShapeDtypeStruct((2, ROWS, COLS), jnp.bfloat16),
        in_specs=[scalars, scalars] + [anywhere] * (n_a + n_b),
        out_specs=pl.BlockSpec(memory_space=pltpu.VMEM),
        scratch_shapes=[
            pltpu.VMEM((16, 2, ROWS, COLS), jnp.bfloat16),
            pltpu.VMEM((16, 2, UNIT, COLS), jnp.bfloat16),
            pltpu.VMEM((2, ROWS, COLS), jnp.float32),
            pltpu.SemaphoreType.DMA((16,)),
            pltpu.SemaphoreType.DMA((16,)),
        ],
        compiler_params=pltpu.CompilerParams(vmem_limit_bytes=VMEM_LIMIT),
        cost_estimate=pl.CostEstimate(
            flops=2 * 2 * ROWS * COLS * 8 * ROWS, bytes_accessed=25 * 2**20, transcendentals=0
        ),
    )(place, keep, *a_arrays, *b_arrays)


def work(density, density_mask, response, response_mask, filter_mask):
    place = jnp.stack([lax.axis_index("row"), lax.axis_index("col")]).astype(jnp.int32)
    (own,) = masked(density, density_mask)
    b0, b0a, b0b = masked(response, response_mask)

    p0o, across = other_core(own), across_x(own)
    q0 = jnp.stack([across, other_core(across)])
    p1a, p1b = along_z(own), along_z(p0o)
    p2a, p2b = along_z(p1a), along_z(p1b)
    p3a, p3b = along_z(p2a), along_z(p2b)
    p1ao, p1bo = other_core(p1a), other_core(p1b)
    p2ao, p2bo = other_core(p2a), other_core(p2b)
    p3ao, p3bo = other_core(p3a), other_core(p3b)
    p4 = along_z(p3a)
    p4o = other_core(p4)
    q3a, q3b = across_x(p3a), across_x(p3b)
    q3ao, q3bo = other_core(q3a), other_core(q3b)
    q1 = along_z(q0)
    q2 = along_z(q1)
    q1o, q2o = other_core(q1), other_core(q2)
    q4 = along_z(q3a)
    q4o = other_core(q4)

    r1 = along_y(b0)
    r2 = along_y(r1)
    r3 = along_y(r2)
    s0a, s0b = beside_x(b0a), beside_x(b0b)
    s1a, s1b = along_y(s0a), along_y(s0b)
    s2a, s2b = along_y(s1a), along_y(s1b)
    s3a, s3b = along_y(s2a), along_y(s2b)

    both = lambda v: [(v, 0), (v, 1)]
    two = lambda v, w: [(v, None), (w, None)]
    units = [
        two(own, p0o), both(q0),
        two(p1ao, p1bo), both(q1o),
        two(p2ao, p2bo), both(q2o),
        two(p3ao, p3bo), two(q3ao, q3bo),
        two(p4, p4o), two(q4, q4o),
        two(p3a, p3b), two(q3a, q3b),
        two(p2a, p2b), both(q2),
        two(p1a, p1b), both(q1),
    ]
    b_parts = [(v, None, i, 0) for i, v in enumerate([b0, r1, r2, r3])]
    for i, pair in enumerate([(s0a, s0b), (s1a, s1b), (s2a, s2b), (s3a, s3b)]):
        b_parts += [(v, d, i, 1) for d, v in enumerate(pair)]
    return multiply(place, jnp.swapaxes(filter_mask, 0, 1), units, b_parts)


def solution(mesh):
    in_specs = (
        P("row", "col"),
        P("row", "col"),
        P(None, "row", "col"),
        P(None, "row", "col"),
        P("row", "col"),
    )
    out_specs = P(None, "row", "col")
    return jax.shard_map(work, mesh=mesh, in_specs=in_specs, out_specs=out_specs, check_vma=False)
```

time: 236 us -> 148 us (0.63)
  waiting for transfers between devices: 180 us -> 68.3 us
  starting transfers between devices: 6.07 us -> 57.6 us
  Pallas kernels: 0 us -> 18 us
  local copies, waits for them, and re-layouts: 16.4 us -> 0.89 us
  matrix products: 14.8 us -> 0 us
  between operations: 13.5 us -> 0.4 us
  other arithmetic: 4.77 us -> 0.7 us
    all_to_all x1 -> x0, waiting for transfers between devices: 136 us -> none  [sent_to_all(): lax.all_to_all(jnp.broadcast_to(array[None], (peers, *array.shape)), axis...]
    ppermute x0 -> x38, waiting for transfers between devices: none -> 68.3 us  [the longest x9 24.7 us: along_y(): return lax.ppermute(v, ('row', 'col'), pairs)]
    ppermute x0 -> x38, starting transfers between devices: none -> 57.6 us  [the longest x10 20.6 us: along_z(): lax.ppermute(v, 'col', col_pairs(lambda z, hi, core: (z + 1 - 2 * core, h...]
    all_gather x1 -> x0, waiting for transfers between devices: 44.4 us -> none  [body(): density_full = lax.all_gather(masked_density, 'col', axis=1, tiled=True)]
    pallas_call x0 -> x3, Pallas kernels: none -> 18 us  [the longest x1 13.3 us: multiply(): pl.pallas_call(functools.partial(matmul_kernel, n_a, parts, n_b, pieces),...]
    dot_general x1 -> x0, matrix products: 14.8 us -> none  [body(): jnp.einsum('ik,dkj->dij', density_full, gather_directly(masked_response,...]
    reshape x1 -> x0, local copies, waits for them, and re-layouts: 8.04 us -> none  [in_order(): return jnp.moveaxis(tiles, 0, dim).reshape(dims)]
    all_to_all x1 -> x0, starting transfers between devices: 6.07 us -> none  [sent_to_all(): lax.all_to_all(jnp.broadcast_to(array[None], (peers, *array.shape)), axis...]
  transfers between devices with their start and end apart: 2 -> 38, of which waited for: 2 -> 15; matrix products, arithmetic and copies ran while one was open for 7% -> 0% of each run, Pallas kernels for 0% -> 2%
where the time goes in v1:
time: 148 us; the launch traced here: 146 us
  waiting for transfers between devices  68.3 us (46%)
  starting transfers between devices  57.6 us (39%)
  Pallas kernels  18 us (12%)
    ppermute x9, waiting for transfers between devices, along_y(): return lax.ppermute(v, ('row', 'col'), pairs)  24.7 us
    ppermute x10, starting transfers between devices, along_z(): lax.ppermute(v, 'col', col_pairs(lambda z, hi, core: (z + 1 - 2 * core, h...  20.6 us
    ppermute x14, starting transfers between devices, other_core(): lax.ppermute(v, 'col', col_pairs(lambda z, hi, core: (z, hi, core + 1)))  18.8 us
    ppermute x2, waiting for transfers between devices, beside_x(): return lax.ppermute(v, 'row', [(r, r ^ 1) for r in range(8)])  17.2 us
    ppermute x3, waiting for transfers between devices, across_x(): lax.ppermute(v, 'col', col_pairs(lambda z, hi, core: (z, hi + 1, core)))  14 us
    pallas_call x1, Pallas kernels, multiply(): pl.pallas_call(functools.partial(matmul_kernel, n_a, parts, n_b, pieces),...  13.3 us
    ppermute x10, waiting for transfers between devices, along_z(): lax.ppermute(v, 'col', col_pairs(lambda z, hi, core: (z + 1 - 2 * core, h...  11.2 us
    ppermute x9, starting transfers between devices, along_y(): return lax.ppermute(v, ('row', 'col'), pairs)  10.6 us
  transfers between devices with their start and end apart: 38, of which 15 were waited for; matrix products, arithmetic and copies ran while one was open for 0% of the time, Pallas kernels for 2%

profile of v1, /device:TPU:1, one launch (start us, length us, event | category | flops | bytes accessed | tf_op | source)
XLA Modules:
  0.0 145.9 jit_solution(5325357469801474353)
XLA Ops:
  0.0 2.0 %shard_map.55.refs_0_ = bf16[1024,256]{1,0:T(8,128)(2,1)} custom-call(s32[2,8]{1,0:T(2,128)} %bitcast.10, bf16[1024,256]{1,0:T(8,128)(2,1)} %values.2), custom_call_target="tpu_custom_call" | custom-call | flops 1000000 | bytes 1048576 | tf_op jit(solution)/shard_map/pallas_call | solution.py:69
  2.0 6.4 %collective-permute-start.3 = (bf16[1024,256]{1,0:T(8,128)(2,1)}, bf16[1024,256]{1,0:T(8,128)(2,1)S(1)}, u32[]{:S(2)}, u32[]{:S(2)}) collective-permute-start(bf16[1024,256]{1,0:T(8,128)(2,1)} %shard_map.55.refs_0_), channel_id=1, source_target_pairs={{0,4},{1,29},{2,6},{3,31},{4,8},{5,1},{6,10},{7,3},{8,12},{9,5},{1... | collective-permute-start | bytes 1572872 | tf_op jit(solution)/shard_map/ppermute | solution.py:29
  8.4 2.7 %collective-permute-start.1 = (bf16[1024,256]{1,0:T(8,128)(2,1)}, bf16[1024,256]{1,0:T(8,128)(2,1)S(1)}, u32[]{:S(2)}, u32[]{:S(2)}) collective-permute-start(bf16[1024,256]{1,0:T(8,128)(2,1)} %shard_map.55.refs_0_), channel_id=1, source_target_pairs={{0,2},{1,3},{2,0},{3,1},{4,6},{5,7},{6,4},{7,5},{8,10},{9,11},{10,... | collective-permute-start | bytes 1572872 | tf_op jit(solution)/shard_map/ppermute | solution.py:33
  11.1 2.8 %shard_map.56 = (bf16[2,1024,256]{2,1,0:T(8,128)(2,1)}, bf16[1024,256]{1,0:T(8,128)(2,1)}, bf16[1024,256]{1,0:T(8,128)(2,1)}) custom-call(s32[2,2,8]{2,1,0:T(2,128)} %bitcast.9, bf16[2,1024,256]{2,1,0:T(8,128)(2,1)} %values.3), custom_call_target="tpu_custom_call" | custom-call | flops 1000000 | bytes 1048576 | tf_op jit(solution)/shard_map/pallas_call | solution.py:69
  13.9 0.3 collective-permute-start.30
  14.2 1.2 collective-permute-start.31
  15.4 2.7 %collective-permute-start.9 = (bf16[1024,256]{1,0:T(8,128)(2,1)S(1)}, bf16[1024,256]{1,0:T(8,128)(2,1)S(1)}, u32[]{:S(2)}, u32[]{:S(2)}) collective-permute-start(bf16[1024,256]{1,0:T(8,128)(2,1)S(1)} %collective-permute-done.3.refs_24_), channel_id=1, source_target_pairs={{0,4},{1,29},{2,6},{3,31},{4,8},{5,1},{6,10},{7,3},{8,12},{9,5},{1... | collective-permute-start | bytes 1572872 | tf_op jit(solution)/shard_map/ppermute | solution.py:29
  18.1 5.6 %collective-permute-done.1 = bf16[1024,256]{1,0:T(8,128)(2,1)S(1)} collective-permute-done((bf16[1024,256]{1,0:T(8,128)(2,1)}, bf16[1024,256]{1,0:T(8,128)(2,1)S(1)}, u32[]{:S(2)}, u32[]{:S(2)}) %collective-permute-start.1) | collective-permute-done | bytes 524320 | tf_op jit(solution)/shard_map/ppermute | solution.py:33
  23.7 2.8 %collective-permute-start.27 = (bf16[2,1024,256]{2,1,0:T(8,128)(2,1)}, bf16[2,1024,256]{2,1,0:T(8,128)(2,1)S(1)}, u32[]{:S(2)}, u32[]{:S(2)}) collective-permute-start(bf16[2,1024,256]{2,1,0:T(8,128)(2,1)} %get-tuple-element.8.refs_27_), channel_id=1, source_target_pairs={{0,64},{1,193},{2,66},{3,195},{4,68},{5,197},{6,70},{7,199},{8,72}... | collective-permute-start | bytes 3145736 | tf_op jit(solution)/shard_map/ppermute | solution.py:46
  26.5 8.8 %collective-permute-done.30.refs_31_ = bf16[1024,256]{1,0:T(8,128)(2,1)S(1)} collective-permute-done((bf16[1024,256]{1,0:T(8,128)(2,1)}, bf16[1024,256]{1,0:T(8,128)(2,1)S(1)}, u32[]{:S(2)}, u32[]{:S(2)}) %collective-permute-start.30) | collective-permute-done | bytes 524320 | tf_op jit(solution)/shard_map/ppermute | solution.py:50
  35.3 8.4 %collective-permute-done.31.refs_32_ = bf16[1024,256]{1,0:T(8,128)(2,1)S(1)} collective-permute-done((bf16[1024,256]{1,0:T(8,128)(2,1)}, bf16[1024,256]{1,0:T(8,128)(2,1)S(1)}, u32[]{:S(2)}, u32[]{:S(2)}) %collective-permute-start.31) | collective-permute-done | bytes 524320 | tf_op jit(solution)/shard_map/ppermute | solution.py:50
  43.8 3.1 %collective-permute-start.5 = (bf16[1024,256]{1,0:T(8,128)(2,1)S(1)}, bf16[1024,256]{1,0:T(8,128)(2,1)S(1)}, u32[]{:S(2)}, u32[]{:S(2)}) collective-permute-start(bf16[1024,256]{1,0:T(8,128)(2,1)S(1)} %collective-permute-done.refs_1_), channel_id=1, source_target_pairs={{0,4},{1,29},{2,6},{3,31},{4,8},{5,1},{6,10},{7,3},{8,12},{9,5},{1... | collective-permute-start | bytes 1572872 | tf_op jit(solution)/shard_map/ppermute | solution.py:29
  46.9 2.7 %collective-permute-start.32 = (bf16[1024,256]{1,0:T(8,128)(2,1)S(1)}, bf16[1024,256]{1,0:T(8,128)(2,1)S(1)}, u32[]{:S(2)}, u32[]{:S(2)}) collective-permute-start(bf16[1024,256]{1,0:T(8,128)(2,1)S(1)} %collective-permute-done.30.refs_31_), channel_id=1, source_target_pairs={{0,64},{1,193},{2,66},{3,195},{4,68},{5,197},{6,70},{7,199},{8,72}... | collective-permute-start | bytes 1572872 | tf_op jit(solution)/shard_map/ppermute | solution.py:46
  49.6 0.5 collective-permute-start.33
  50.2 2.8 %collective-permute-done.5.refs_25_ = bf16[1024,256]{1,0:T(8,128)(2,1)S(1)} collective-permute-done((bf16[1024,256]{1,0:T(8,128)(2,1)S(1)}, bf16[1024,256]{1,0:T(8,128)(2,1)S(1)}, u32[]{:S(2)}, u32[]{:S(2)}) %collective-permute-start.5) | collective-permute-done | bytes 524320 | tf_op jit(solution)/shard_map/ppermute | solution.py:29
  53.0 2.1 %collective-permute-start.10 = (bf16[1024,256]{1,0:T(8,128)(2,1)S(1)}, bf16[1024,256]{1,0:T(8,128)(2,1)S(1)}, u32[]{:S(2)}, u32[]{:S(2)}) collective-permute-start(bf16[1024,256]{1,0:T(8,128)(2,1)S(1)} %collective-permute-done.9.refs_21_), channel_id=1, source_target_pairs={{0,1},{1,0},{2,3},{3,2},{4,5},{5,4},{6,7},{7,6},{8,9},{9,8},{10,11... | collective-permute-start | bytes 1572872 | tf_op jit(solution)/shard_map/ppermute | solution.py:37
  55.1 0.6 collective-permute-done.32.refs_33_
  55.8 1.1 collective-permute-start.11
  56.9 4.5 %collective-permute-done.33.refs_34_ = bf16[1024,256]{1,0:T(8,128)(2,1)S(1)} collective-permute-done((bf16[1024,256]{1,0:T(8,128)(2,1)S(1)}, bf16[1024,256]{1,0:T(8,128)(2,1)S(1)}, u32[]{:S(2)}, u32[]{:S(2)}) %collective-permute-start.33) | collective-permute-done | bytes 524320 | tf_op jit(solution)/shard_map/ppermute | solution.py:46
  61.4 3.5 %collective-permute-start.34 = (bf16[1024,256]{1,0:T(8,128)(2,1)S(1)}, bf16[1024,256]{1,0:T(8,128)(2,1)S(1)}, u32[]{:S(2)}, u32[]{:S(2)}) collective-permute-start(bf16[1024,256]{1,0:T(8,128)(2,1)S(1)} %collective-permute-done.32.refs_33_), channel_id=1, source_target_pairs={{0,64},{1,193},{2,66},{3,195},{4,68},{5,197},{6,70},{7,199},{8,72}... | collective-permute-start | bytes 1572872 | tf_op jit(solution)/shard_map/ppermute | solution.py:46
  64.9 0.3 collective-permute-start.35
  65.4 0.7 collective-permute-start.7
  66.1 1.7 %collective-permute-start.23 = (bf16[1024,256]{1,0:T(8,128)(2,1)S(1)}, bf16[1024,256]{1,0:T(8,128)(2,1)S(1)}, u32[]{:S(2)}, u32[]{:S(2)}) collective-permute-start(bf16[1024,256]{1,0:T(8,128)(2,1)S(1)} %collective-permute-done.15.refs_17_), channel_id=1, source_target_pairs={{0,4},{1,29},{2,6},{3,31},{4,8},{5,1},{6,10},{7,3},{8,12},{9,5},{1... | collective-permute-start | bytes 1572872 | tf_op jit(solution)/shard_map/ppermute | solution.py:29
  67.7 1.7 %collective-permute-start.19 = (bf16[1024,256]{1,0:T(8,128)(2,1)S(1)}, bf16[1024,256]{1,0:T(8,128)(2,1)S(1)}, u32[]{:S(2)}, u32[]{:S(2)}) collective-permute-start(bf16[1024,256]{1,0:T(8,128)(2,1)S(1)} %collective-permute-done.15.refs_17_), channel_id=1, source_target_pairs={{0,2},{1,3},{2,0},{3,1},{4,6},{5,7},{6,4},{7,5},{8,10},{9,11},{10,... | collective-permute-start | bytes 1572872 | tf_op jit(solution)/shard_map/ppermute | solution.py:33
  69.5 1.5 %collective-permute-done.34.refs_35_ = bf16[1024,256]{1,0:T(8,128)(2,1)S(1)} collective-permute-done((bf16[1024,256]{1,0:T(8,128)(2,1)S(1)}, bf16[1024,256]{1,0:T(8,128)(2,1)S(1)}, u32[]{:S(2)}, u32[]{:S(2)}) %collective-permute-start.34) | collective-permute-done | bytes 524320 | tf_op jit(solution)/shard_map/ppermute | solution.py:46
  71.0 1.7 %collective-permute-start.16 = (bf16[1024,256]{1,0:T(8,128)(2,1)S(1)}, bf16[1024,256]{1,0:T(8,128)(2,1)S(1)}, u32[]{:S(2)}, u32[]{:S(2)}) collective-permute-start(bf16[1024,256]{1,0:T(8,128)(2,1)S(1)} %collective-permute-done.15.refs_17_), channel_id=1, source_target_pairs={{0,1},{1,0},{2,3},{3,2},{4,5},{5,4},{6,7},{7,6},{8,9},{9,8},{10,11... | collective-permute-start | bytes 1572872 | tf_op jit(solution)/shard_map/ppermute | solution.py:37
  72.7 3.9 %collective-permute-done.35.refs_36_ = bf16[1024,256]{1,0:T(8,128)(2,1)S(1)} collective-permute-done((bf16[1024,256]{1,0:T(8,128)(2,1)S(1)}, bf16[1024,256]{1,0:T(8,128)(2,1)S(1)}, u32[]{:S(2)}, u32[]{:S(2)}) %collective-permute-start.35) | collective-permute-done | bytes 524320 | tf_op jit(solution)/shard_map/ppermute | solution.py:46
  76.6 1.2 collective-permute-start.17
  77.9 7.1 %collective-permute-done.23.refs_13_ = bf16[1024,256]{1,0:T(8,128)(2,1)S(1)} collective-permute-done((bf16[1024,256]{1,0:T(8,128)(2,1)S(1)}, bf16[1024,256]{1,0:T(8,128)(2,1)S(1)}, u32[]{:S(2)}, u32[]{:S(2)}) %collective-permute-start.23) | collective-permute-done | bytes 524320 | tf_op jit(solution)/shard_map/ppermute | solution.py:29
  85.0 3.9 %collective-permute-start.12 = (bf16[1024,256]{1,0:T(8,128)(2,1)S(1)}, bf16[1024,256]{1,0:T(8,128)(2,1)S(1)}, u32[]{:S(2)}, u32[]{:S(2)}) collective-permute-start(bf16[1024,256]{1,0:T(8,128)(2,1)S(1)} %collective-permute-done.11.refs_22_), channel_id=1, source_target_pairs={{0,1},{1,0},{2,3},{3,2},{4,5},{5,4},{6,7},{7,6},{8,9},{9,8},{10,11... | collective-permute-start | bytes 1572872 | tf_op jit(solution)/shard_map/ppermute | solution.py:37
  88.9 0.5 collective-permute-start.36
  89.4 1.2 collective-permute-done.17.refs_18_
  90.7 2.0 %collective-permute-start.13 = (bf16[2,1024,256]{2,1,0:T(8,128)(2,1)}, bf16[2,1024,256]{2,1,0:T(8,128)(2,1)}, u32[]{:S(2)}, u32[]{:S(2)}) collective-permute-start(bf16[2,1024,256]{2,1,0:T(8,128)(2,1)} %collective-permute-done.7.refs_26_), channel_id=1, source_target_pairs={{0,4},{1,29},{2,6},{3,31},{4,8},{5,1},{6,10},{7,3},{8,12},{9,5},{1... | collective-permute-start | bytes 3145736 | tf_op jit(solution)/shard_map/ppermute | solution.py:29
  92.7 2.0 %collective-permute-start.24 = (bf16[1024,256]{1,0:T(8,128)(2,1)S(1)}, bf16[1024,256]{1,0:T(8,128)(2,1)S(1)}, u32[]{:S(2)}, u32[]{:S(2)}) collective-permute-start(bf16[1024,256]{1,0:T(8,128)(2,1)S(1)} %collective-permute-done.23.refs_13_), channel_id=1, source_target_pairs={{0,1},{1,0},{2,3},{3,2},{4,5},{5,4},{6,7},{7,6},{8,9},{9,8},{10,11... | collective-permute-start | bytes 1572872 | tf_op jit(solution)/shard_map/ppermute | solution.py:37
  94.6 10.0 %collective-permute-done.36.refs_37_ = bf16[1024,256]{1,0:T(8,128)(2,1)S(1)} collective-permute-done((bf16[1024,256]{1,0:T(8,128)(2,1)S(1)}, bf16[1024,256]{1,0:T(8,128)(2,1)S(1)}, u32[]{:S(2)}, u32[]{:S(2)}) %collective-permute-start.36) | collective-permute-done | bytes 524320 | tf_op jit(solution)/shard_map/ppermute | solution.py:46
  104.7 1.5 %collective-permute-start.25 = (bf16[1024,256]{1,0:T(8,128)(2,1)S(1)}, bf16[1024,256]{1,0:T(8,128)(2,1)}, u32[]{:S(2)}, u32[]{:S(2)}) collective-permute-start(bf16[1024,256]{1,0:T(8,128)(2,1)S(1)} %collective-permute-done.19.refs_19_), channel_id=1, source_target_pairs={{0,4},{1,29},{2,6},{3,31},{4,8},{5,1},{6,10},{7,3},{8,12},{9,5},{1... | collective-permute-start | bytes 1572872 | tf_op jit(solution)/shard_map/ppermute | solution.py:29
  106.2 4.1 %collective-permute-done.37.refs_38_ = bf16[1024,256]{1,0:T(8,128)(2,1)S(1)} collective-permute-done((bf16[1024,256]{1,0:T(8,128)(2,1)S(1)}, bf16[1024,256]{1,0:T(8,128)(2,1)S(1)}, u32[]{:S(2)}, u32[]{:S(2)}) %collective-permute-start.37) | collective-permute-done | bytes 524320 | tf_op jit(solution)/shard_map/ppermute | solution.py:46
  110.3 3.4 %collective-permute-start.20 = (bf16[1024,256]{1,0:T(8,128)(2,1)S(1)}, bf16[1024,256]{1,0:T(8,128)(2,1)S(1)}, u32[]{:S(2)}, u32[]{:S(2)}) collective-permute-start(bf16[1024,256]{1,0:T(8,128)(2,1)S(1)} %collective-permute-done.19.refs_19_), channel_id=1, source_target_pairs={{0,1},{1,0},{2,3},{3,2},{4,5},{5,4},{6,7},{7,6},{8,9},{9,8},{10,11... | collective-permute-start | bytes 1572872 | tf_op jit(solution)/shard_map/ppermute | solution.py:37
  113.8 1.7 %collective-permute-start.21 = (bf16[1024,256]{1,0:T(8,128)(2,1)S(1)}, bf16[1024,256]{1,0:T(8,128)(2,1)}, u32[]{:S(2)}, u32[]{:S(2)}) collective-permute-start(bf16[1024,256]{1,0:T(8,128)(2,1)S(1)} %collective-permute-done.17.refs_18_), channel_id=1, source_target_pairs={{0,2},{1,3},{2,0},{3,1},{4,6},{5,7},{6,4},{7,5},{8,10},{9,11},{10,... | collective-permute-start | bytes 1572872 | tf_op jit(solution)/shard_map/ppermute | solution.py:33
  115.5 0.2 collective-permute-start.29
  115.8 4.2 %collective-permute-start.18 = (bf16[1024,256]{1,0:T(8,128)(2,1)S(1)}, bf16[1024,256]{1,0:T(8,128)(2,1)S(1)}, u32[]{:S(2)}, u32[]{:S(2)}) collective-permute-start(bf16[1024,256]{1,0:T(8,128)(2,1)S(1)} %collective-permute-done.17.refs_18_), channel_id=1, source_target_pairs={{0,1},{1,0},{2,3},{3,2},{4,5},{5,4},{6,7},{7,6},{8,9},{9,8},{10,11... | collective-permute-start | bytes 1572872 | tf_op jit(solution)/shard_map/ppermute | solution.py:37
  120.1 8.4 %collective-permute-done.21.refs_20_ = bf16[1024,256]{1,0:T(8,128)(2,1)} collective-permute-done((bf16[1024,256]{1,0:T(8,128)(2,1)S(1)}, bf16[1024,256]{1,0:T(8,128)(2,1)}, u32[]{:S(2)}, u32[]{:S(2)}) %collective-permute-start.21) | collective-permute-done | bytes 524320 | tf_op jit(solution)/shard_map/ppermute | solution.py:33
  128.5 1.3 collective-permute-start.26
  129.9 0.6 copy-done.28
  130.6 0.6 pad_add_fusion.place
  131.2 0.4 collective-permute-done.26.refs_16_
  131.6 0.7 collective-permute-done.22.refs_12_
  132.5 13.3 %shard_map.57 = bf16[2,1024,256]{2,1,0:T(8,128)(2,1)} custom-call(s32[2]{0:T(128)} %pad_add_fusion.place, s32[2,8]{1,0:T(2,128)} %bitcast.11, bf16[1024,256]{1,0:T(8,128)(2,1)} %shard_map.55.refs_0_, bf16[1024,256]{1,0:T(8,128)(2,1)} %copy-done.5, bf16[2,1024,256]{2,1,0:T(8,128)(2,1)} %copy-done, bf16[1024,256]{1,0:T(8,128)(2,1)} %copy-done.9, ...), custom_call_target="tpu_custom_call" | custom-call | flops 8589934592 | bytes 26214400 | tf_op jit(solution)/shard_map/pallas_call | solution.py:162
  (91 shorter events, 0.9 us)
Async XLA Ops:
  2.0 13.4 %collective-permute-start.3 = (bf16[1024,256]{1,0:T(8,128)(2,1)}, bf16[1024,256]{1,0:T(8,128)(2,1)S(1)}, u32[]{:S(2)}, u32[]{:S(2)}) collective-permute-start(bf16[1024,256]{1,0:T(8,128)(2,1)} %shard_map.55.refs_0_), channel_id=1, source_target_pairs={{0,4},{1,29},{2,6},{3,31},{4,8},{5,1},{6,10},{7,3},{8,12},{9,5},{1... | collective-permute-start | bytes 1572872 | tf_op jit(solution)/shard_map/ppermute | solution.py:29
  8.4 15.4 %collective-permute-start.1 = (bf16[1024,256]{1,0:T(8,128)(2,1)}, bf16[1024,256]{1,0:T(8,128)(2,1)S(1)}, u32[]{:S(2)}, u32[]{:S(2)}) collective-permute-start(bf16[1024,256]{1,0:T(8,128)(2,1)} %shard_map.55.refs_0_), channel_id=1, source_target_pairs={{0,2},{1,3},{2,0},{3,1},{4,6},{5,7},{6,4},{7,5},{8,10},{9,11},{10,... | collective-permute-start | bytes 1572872 | tf_op jit(solution)/shard_map/ppermute | solution.py:33
  11.1 12.6 %collective-permute-start = (bf16[1024,256]{1,0:T(8,128)(2,1)}, bf16[1024,256]{1,0:T(8,128)(2,1)S(1)}, u32[]{:S(2)}, u32[]{:S(2)}) collective-permute-start(bf16[1024,256]{1,0:T(8,128)(2,1)} %shard_map.55.refs_0_), channel_id=1, source_target_pairs={{0,1},{1,0},{2,3},{3,2},{4,5},{5,4},{6,7},{7,6},{8,9},{9,8},{10,11... | collective-permute-start | bytes 1572872 | tf_op jit(solution)/shard_map/ppermute | solution.py:37
  13.9 21.4 %collective-permute-start.30 = (bf16[1024,256]{1,0:T(8,128)(2,1)}, bf16[1024,256]{1,0:T(8,128)(2,1)S(1)}, u32[]{:S(2)}, u32[]{:S(2)}) collective-permute-start(bf16[1024,256]{1,0:T(8,128)(2,1)} %get-tuple-element.9), channel_id=1, source_target_pairs={{0,32},{32,0},{64,96},{96,64},{128,160},{160,128},{192,224},{224,1... | collective-permute-start | bytes 1572872 | tf_op jit(solution)/shard_map/ppermute | solution.py:50
  14.2 29.5 %collective-permute-start.31 = (bf16[1024,256]{1,0:T(8,128)(2,1)}, bf16[1024,256]{1,0:T(8,128)(2,1)S(1)}, u32[]{:S(2)}, u32[]{:S(2)}) collective-permute-start(bf16[1024,256]{1,0:T(8,128)(2,1)} %get-tuple-element.10), channel_id=1, source_target_pairs={{0,32},{32,0},{64,96},{96,64},{128,160},{160,128},{192,224},{224,1... | collective-permute-start | bytes 1572872 | tf_op jit(solution)/shard_map/ppermute | solution.py:50
  15.4 49.8 %copy-start.4 = (bf16[1024,256]{1,0:T(8,128)(2,1)}, bf16[1024,256]{1,0:T(8,128)(2,1)S(1)}, u32[]{:S(2)}) copy-start(bf16[1024,256]{1,0:T(8,128)(2,1)S(1)} %collective-permute-done.3.refs_24_) | copy-start | bytes 1572868
  15.4 31.5 %collective-permute-start.9 = (bf16[1024,256]{1,0:T(8,128)(2,1)S(1)}, bf16[1024,256]{1,0:T(8,128)(2,1)S(1)}, u32[]{:S(2)}, u32[]{:S(2)}) collective-permute-start(bf16[1024,256]{1,0:T(8,128)(2,1)S(1)} %collective-permute-done.3.refs_24_), channel_id=1, source_target_pairs={{0,4},{1,29},{2,6},{3,31},{4,8},{5,1},{6,10},{7,3},{8,12},{9,5},{1... | collective-permute-start | bytes 1572872 | tf_op jit(solution)/shard_map/ppermute | solution.py:29
  23.7 25.9 %collective-permute-start.4 = (bf16[1024,256]{1,0:T(8,128)(2,1)S(1)}, bf16[1024,256]{1,0:T(8,128)(2,1)S(1)}, u32[]{:S(2)}, u32[]{:S(2)}) collective-permute-start(bf16[1024,256]{1,0:T(8,128)(2,1)S(1)} %collective-permute-done.3.refs_24_), channel_id=1, source_target_pairs={{0,1},{1,0},{2,3},{3,2},{4,5},{5,4},{6,7},{7,6},{8,9},{9,8},{10,11... | collective-permute-start | bytes 1572872 | tf_op jit(solution)/shard_map/ppermute | solution.py:37
  23.7 37.7 %collective-permute-start.27 = (bf16[2,1024,256]{2,1,0:T(8,128)(2,1)}, bf16[2,1024,256]{2,1,0:T(8,128)(2,1)S(1)}, u32[]{:S(2)}, u32[]{:S(2)}) collective-permute-start(bf16[2,1024,256]{2,1,0:T(8,128)(2,1)} %get-tuple-element.8.refs_27_), channel_id=1, source_target_pairs={{0,64},{1,193},{2,66},{3,195},{4,68},{5,197},{6,70},{7,199},{8,72}... | collective-permute-start | bytes 3145736 | tf_op jit(solution)/shard_map/ppermute | solution.py:46
  35.3 14.8 %collective-permute-start.2 = (bf16[1024,256]{1,0:T(8,128)(2,1)S(1)}, bf16[1024,256]{1,0:T(8,128)(2,1)S(1)}, u32[]{:S(2)}, u32[]{:S(2)}) collective-permute-start(bf16[1024,256]{1,0:T(8,128)(2,1)S(1)} %collective-permute-done.1), channel_id=1, source_target_pairs={{0,1},{1,0},{2,3},{3,2},{4,5},{5,4},{6,7},{7,6},{8,9},{9,8},{10,11... | collective-permute-start | bytes 1572872 | tf_op jit(solution)/shard_map/ppermute | solution.py:37
  43.8 9.3 %collective-permute-start.5 = (bf16[1024,256]{1,0:T(8,128)(2,1)S(1)}, bf16[1024,256]{1,0:T(8,128)(2,1)S(1)}, u32[]{:S(2)}, u32[]{:S(2)}) collective-permute-start(bf16[1024,256]{1,0:T(8,128)(2,1)S(1)} %collective-permute-done.refs_1_), channel_id=1, source_target_pairs={{0,4},{1,29},{2,6},{3,31},{4,8},{5,1},{6,10},{7,3},{8,12},{9,5},{1... | collective-permute-start | bytes 1572872 | tf_op jit(solution)/shard_map/ppermute | solution.py:29
  46.9 8.9 %collective-permute-start.32 = (bf16[1024,256]{1,0:T(8,128)(2,1)S(1)}, bf16[1024,256]{1,0:T(8,128)(2,1)S(1)}, u32[]{:S(2)}, u32[]{:S(2)}) collective-permute-start(bf16[1024,256]{1,0:T(8,128)(2,1)S(1)} %collective-permute-done.30.refs_31_), channel_id=1, source_target_pairs={{0,64},{1,193},{2,66},{3,195},{4,68},{5,197},{6,70},{7,199},{8,72}... | collective-permute-start | bytes 1572872 | tf_op jit(solution)/shard_map/ppermute | solution.py:46
  49.6 11.7 %collective-permute-start.33 = (bf16[1024,256]{1,0:T(8,128)(2,1)S(1)}, bf16[1024,256]{1,0:T(8,128)(2,1)S(1)}, u32[]{:S(2)}, u32[]{:S(2)}) collective-permute-start(bf16[1024,256]{1,0:T(8,128)(2,1)S(1)} %collective-permute-done.31.refs_32_), channel_id=1, source_target_pairs={{0,64},{1,193},{2,66},{3,195},{4,68},{5,197},{6,70},{7,199},{8,72}... | collective-permute-start | bytes 1572872 | tf_op jit(solution)/shard_map/ppermute | solution.py:46
  50.1 14.8 %collective-permute-start.15 = (bf16[1024,256]{1,0:T(8,128)(2,1)S(1)}, bf16[1024,256]{1,0:T(8,128)(2,1)S(1)}, u32[]{:S(2)}, u32[]{:S(2)}) collective-permute-start(bf16[1024,256]{1,0:T(8,128)(2,1)S(1)} %collective-permute-done.9.refs_21_), channel_id=1, source_target_pairs={{0,4},{1,29},{2,6},{3,31},{4,8},{5,1},{6,10},{7,3},{8,12},{9,5},{1... | collective-permute-start | bytes 1572872 | tf_op jit(solution)/shard_map/ppermute | solution.py:29
  53.0 12.3 %collective-permute-start.10 = (bf16[1024,256]{1,0:T(8,128)(2,1)S(1)}, bf16[1024,256]{1,0:T(8,128)(2,1)S(1)}, u32[]{:S(2)}, u32[]{:S(2)}) collective-permute-start(bf16[1024,256]{1,0:T(8,128)(2,1)S(1)} %collective-permute-done.9.refs_21_), channel_id=1, source_target_pairs={{0,1},{1,0},{2,3},{3,2},{4,5},{5,4},{6,7},{7,6},{8,9},{9,8},{10,11... | collective-permute-start | bytes 1572872 | tf_op jit(solution)/shard_map/ppermute | solution.py:37
  55.8 59.7 %copy-start.11 = (bf16[1024,256]{1,0:T(8,128)(2,1)}, bf16[1024,256]{1,0:T(8,128)(2,1)S(1)}, u32[]{:S(2)}) copy-start(bf16[1024,256]{1,0:T(8,128)(2,1)S(1)} %collective-permute-done.32.refs_33_) | copy-start | bytes 1572868
  55.8 10.3 %collective-permute-start.11 = (bf16[1024,256]{1,0:T(8,128)(2,1)S(1)}, bf16[1024,256]{1,0:T(8,128)(2,1)S(1)}, u32[]{:S(2)}, u32[]{:S(2)}) collective-permute-start(bf16[1024,256]{1,0:T(8,128)(2,1)S(1)} %collective-permute-done.5.refs_25_), channel_id=1, source_target_pairs={{0,4},{1,29},{2,6},{3,31},{4,8},{5,1},{6,10},{7,3},{8,12},{9,5},{1... | collective-permute-start | bytes 1572872 | tf_op jit(solution)/shard_map/ppermute | solution.py:29
  61.4 54.1 %copy-start.12 = (bf16[1024,256]{1,0:T(8,128)(2,1)}, bf16[1024,256]{1,0:T(8,128)(2,1)S(1)}, u32[]{:S(2)}) copy-start(bf16[1024,256]{1,0:T(8,128)(2,1)S(1)} %collective-permute-done.33.refs_34_) | copy-start | bytes 1572868
  61.4 6.4 %collective-permute-start.6 = (bf16[1024,256]{1,0:T(8,128)(2,1)S(1)}, bf16[1024,256]{1,0:T(8,128)(2,1)S(1)}, u32[]{:S(2)}, u32[]{:S(2)}) collective-permute-start(bf16[1024,256]{1,0:T(8,128)(2,1)S(1)} %collective-permute-done.5.refs_25_), channel_id=1, source_target_pairs={{0,1},{1,0},{2,3},{3,2},{4,5},{5,4},{6,7},{7,6},{8,9},{9,8},{10,11... | collective-permute-start | bytes 1572872 | tf_op jit(solution)/shard_map/ppermute | solution.py:37
  61.4 9.6 %collective-permute-start.34 = (bf16[1024,256]{1,0:T(8,128)(2,1)S(1)}, bf16[1024,256]{1,0:T(8,128)(2,1)S(1)}, u32[]{:S(2)}, u32[]{:S(2)}) collective-permute-start(bf16[1024,256]{1,0:T(8,128)(2,1)S(1)} %collective-permute-done.32.refs_33_), channel_id=1, source_target_pairs={{0,64},{1,193},{2,66},{3,195},{4,68},{5,197},{6,70},{7,199},{8,72}... | collective-permute-start | bytes 1572872 | tf_op jit(solution)/shard_map/ppermute | solution.py:46
  64.9 50.9 %copy-start.13 = (bf16[1024,256]{1,0:T(8,128)(2,1)}, bf16[1024,256]{1,0:T(8,128)(2,1)S(1)}, u32[]{:S(2)}) copy-start(bf16[1024,256]{1,0:T(8,128)(2,1)S(1)} %collective-permute-done.15.refs_17_) | copy-start | bytes 1572868
  64.9 11.7 %collective-permute-start.35 = (bf16[1024,256]{1,0:T(8,128)(2,1)S(1)}, bf16[1024,256]{1,0:T(8,128)(2,1)S(1)}, u32[]{:S(2)}, u32[]{:S(2)}) collective-permute-start(bf16[1024,256]{1,0:T(8,128)(2,1)S(1)} %collective-permute-done.33.refs_34_), channel_id=1, source_target_pairs={{0,64},{1,193},{2,66},{3,195},{4,68},{5,197},{6,70},{7,199},{8,72}... | collective-permute-start | bytes 1572872 | tf_op jit(solution)/shard_map/ppermute | solution.py:46
  65.3 67.0 %copy-start = (bf16[2,1024,256]{2,1,0:T(8,128)(2,1)}, bf16[2,1024,256]{2,1,0:T(8,128)(2,1)S(1)}, u32[]{:S(2)}) copy-start(bf16[2,1024,256]{2,1,0:T(8,128)(2,1)S(1)} %pad_maximum_fusion.refs_2_) | copy-start | bytes 3145732
  65.3 50.4 %copy-start.14 = (bf16[1024,256]{1,0:T(8,128)(2,1)}, bf16[1024,256]{1,0:T(8,128)(2,1)S(1)}, u32[]{:S(2)}) copy-start(bf16[1024,256]{1,0:T(8,128)(2,1)S(1)} %collective-permute-done.10.refs_6_) | copy-start | bytes 1572868
  65.4 25.3 %collective-permute-start.7 = (bf16[2,1024,256]{2,1,0:T(8,128)(2,1)S(1)}, bf16[2,1024,256]{2,1,0:T(8,128)(2,1)}, u32[]{:S(2)}, u32[]{:S(2)}) collective-permute-start(bf16[2,1024,256]{2,1,0:T(8,128)(2,1)S(1)} %pad_maximum_fusion.refs_2_), channel_id=1, source_target_pairs={{0,4},{1,29},{2,6},{3,31},{4,8},{5,1},{6,10},{7,3},{8,12},{9,5},{1... | collective-permute-start | bytes 3145736 | tf_op jit(solution)/shard_map/ppermute | solution.py:29
  66.1 53.9 %copy-start.15 = (bf16[1024,256]{1,0:T(8,128)(2,1)}, bf16[1024,256]{1,0:T(8,128)(2,1)S(1)}, u32[]{:S(2)}) copy-start(bf16[1024,256]{1,0:T(8,128)(2,1)S(1)} %collective-permute-done.11.refs_22_) | copy-start | bytes 1572868
  66.1 18.9 %collective-permute-start.23 = (bf16[1024,256]{1,0:T(8,128)(2,1)S(1)}, bf16[1024,256]{1,0:T(8,128)(2,1)S(1)}, u32[]{:S(2)}, u32[]{:S(2)}) collective-permute-start(bf16[1024,256]{1,0:T(8,128)(2,1)S(1)} %collective-permute-done.15.refs_17_), channel_id=1, source_target_pairs={{0,4},{1,29},{2,6},{3,31},{4,8},{5,1},{6,10},{7,3},{8,12},{9,5},{1... | collective-permute-start | bytes 1572872 | tf_op jit(solution)/shard_map/ppermute | solution.py:29
  67.7 52.2 %copy-start.16 = (bf16[1024,256]{1,0:T(8,128)(2,1)}, bf16[1024,256]{1,0:T(8,128)(2,1)S(1)}, u32[]{:S(2)}) copy-start(bf16[1024,256]{1,0:T(8,128)(2,1)S(1)} %collective-permute-done.6.refs_4_) | copy-start | bytes 1572868
  67.7 17.3 %collective-permute-start.19 = (bf16[1024,256]{1,0:T(8,128)(2,1)S(1)}, bf16[1024,256]{1,0:T(8,128)(2,1)S(1)}, u32[]{:S(2)}, u32[]{:S(2)}) collective-permute-start(bf16[1024,256]{1,0:T(8,128)(2,1)S(1)} %collective-permute-done.15.refs_17_), channel_id=1, source_target_pairs={{0,2},{1,3},{2,0},{3,1},{4,6},{5,7},{6,4},{7,5},{8,10},{9,11},{10,... | collective-permute-start | bytes 1572872 | tf_op jit(solution)/shard_map/ppermute | solution.py:33
  71.0 49.1 %copy-start.17 = (bf16[1024,256]{1,0:T(8,128)(2,1)}, bf16[1024,256]{1,0:T(8,128)(2,1)S(1)}, u32[]{:S(2)}) copy-start(bf16[1024,256]{1,0:T(8,128)(2,1)S(1)} %collective-permute-done.34.refs_35_) | copy-start | bytes 1572868
  71.0 17.9 %collective-permute-start.16 = (bf16[1024,256]{1,0:T(8,128)(2,1)S(1)}, bf16[1024,256]{1,0:T(8,128)(2,1)S(1)}, u32[]{:S(2)}, u32[]{:S(2)}) collective-permute-start(bf16[1024,256]{1,0:T(8,128)(2,1)S(1)} %collective-permute-done.15.refs_17_), channel_id=1, source_target_pairs={{0,1},{1,0},{2,3},{3,2},{4,5},{5,4},{6,7},{7,6},{8,9},{9,8},{10,11... | collective-permute-start | bytes 1572872 | tf_op jit(solution)/shard_map/ppermute | solution.py:37
  76.6 51.8 %copy-start.18 = (bf16[1024,256]{1,0:T(8,128)(2,1)}, bf16[1024,256]{1,0:T(8,128)(2,1)S(1)}, u32[]{:S(2)}) copy-start(bf16[1024,256]{1,0:T(8,128)(2,1)S(1)} %collective-permute-done.35.refs_36_) | copy-start | bytes 1572868
  76.6 14.0 %collective-permute-start.17 = (bf16[1024,256]{1,0:T(8,128)(2,1)S(1)}, bf16[1024,256]{1,0:T(8,128)(2,1)S(1)}, u32[]{:S(2)}, u32[]{:S(2)}) collective-permute-start(bf16[1024,256]{1,0:T(8,128)(2,1)S(1)} %collective-permute-done.11.refs_22_), channel_id=1, source_target_pairs={{0,4},{1,29},{2,6},{3,31},{4,8},{5,1},{6,10},{7,3},{8,12},{9,5},{1... | collective-permute-start | bytes 1572872 | tf_op jit(solution)/shard_map/ppermute | solution.py:29
  85.0 28.7 %collective-permute-start.28 = (bf16[2,1024,256]{2,1,0:T(8,128)(2,1)S(1)}, bf16[2,1024,256]{2,1,0:T(8,128)(2,1)}, u32[]{:S(2)}, u32[]{:S(2)}) collective-permute-start(bf16[2,1024,256]{2,1,0:T(8,128)(2,1)S(1)} %collective-permute-done.27.refs_28_), channel_id=1, source_target_pairs={{0,64},{1,193},{2,66},{3,195},{4,68},{5,197},{6,70},{7,199},{8,72}... | collective-permute-start | bytes 3145736 | tf_op jit(solution)/shard_map/ppermute | solution.py:46
  85.0 7.6 %collective-permute-start.12 = (bf16[1024,256]{1,0:T(8,128)(2,1)S(1)}, bf16[1024,256]{1,0:T(8,128)(2,1)S(1)}, u32[]{:S(2)}, u32[]{:S(2)}) collective-permute-start(bf16[1024,256]{1,0:T(8,128)(2,1)S(1)} %collective-permute-done.11.refs_22_), channel_id=1, source_target_pairs={{0,1},{1,0},{2,3},{3,2},{4,5},{5,4},{6,7},{7,6},{8,9},{9,8},{10,11... | collective-permute-start | bytes 1572872 | tf_op jit(solution)/shard_map/ppermute | solution.py:37
  88.9 15.8 %collective-permute-start.36 = (bf16[1024,256]{1,0:T(8,128)(2,1)S(1)}, bf16[1024,256]{1,0:T(8,128)(2,1)S(1)}, u32[]{:S(2)}, u32[]{:S(2)}) collective-permute-start(bf16[1024,256]{1,0:T(8,128)(2,1)S(1)} %collective-permute-done.34.refs_35_), channel_id=1, source_target_pairs={{0,64},{1,193},{2,66},{3,195},{4,68},{5,197},{6,70},{7,199},{8,72}... | collective-permute-start | bytes 1572872 | tf_op jit(solution)/shard_map/ppermute | solution.py:46
  90.6 19.7 %collective-permute-start.37 = (bf16[1024,256]{1,0:T(8,128)(2,1)S(1)}, bf16[1024,256]{1,0:T(8,128)(2,1)S(1)}, u32[]{:S(2)}, u32[]{:S(2)}) collective-permute-start(bf16[1024,256]{1,0:T(8,128)(2,1)S(1)} %collective-permute-done.35.refs_36_), channel_id=1, source_target_pairs={{0,64},{1,193},{2,66},{3,195},{4,68},{5,197},{6,70},{7,199},{8,72}... | collective-permute-start | bytes 1572872 | tf_op jit(solution)/shard_map/ppermute | solution.py:46
  90.7 29.3 %collective-permute-start.13 = (bf16[2,1024,256]{2,1,0:T(8,128)(2,1)}, bf16[2,1024,256]{2,1,0:T(8,128)(2,1)}, u32[]{:S(2)}, u32[]{:S(2)}) collective-permute-start(bf16[2,1024,256]{2,1,0:T(8,128)(2,1)} %collective-permute-done.7.refs_26_), channel_id=1, source_target_pairs={{0,4},{1,29},{2,6},{3,31},{4,8},{5,1},{6,10},{7,3},{8,12},{9,5},{1... | collective-permute-start | bytes 3145736 | tf_op jit(solution)/shard_map/ppermute | solution.py:29
  92.7 21.1 %collective-permute-start.24 = (bf16[1024,256]{1,0:T(8,128)(2,1)S(1)}, bf16[1024,256]{1,0:T(8,128)(2,1)S(1)}, u32[]{:S(2)}, u32[]{:S(2)}) collective-permute-start(bf16[1024,256]{1,0:T(8,128)(2,1)S(1)} %collective-permute-done.23.refs_13_), channel_id=1, source_target_pairs={{0,1},{1,0},{2,3},{3,2},{4,5},{5,4},{6,7},{7,6},{8,9},{9,8},{10,11... | collective-permute-start | bytes 1572872 | tf_op jit(solution)/shard_map/ppermute | solution.py:37
  104.7 10.8 %collective-permute-start.25 = (bf16[1024,256]{1,0:T(8,128)(2,1)S(1)}, bf16[1024,256]{1,0:T(8,128)(2,1)}, u32[]{:S(2)}, u32[]{:S(2)}) collective-permute-start(bf16[1024,256]{1,0:T(8,128)(2,1)S(1)} %collective-permute-done.19.refs_19_), channel_id=1, source_target_pairs={{0,4},{1,29},{2,6},{3,31},{4,8},{5,1},{6,10},{7,3},{8,12},{9,5},{1... | collective-permute-start | bytes 1572872 | tf_op jit(solution)/shard_map/ppermute | solution.py:29
  110.3 5.5 %collective-permute-start.20 = (bf16[1024,256]{1,0:T(8,128)(2,1)S(1)}, bf16[1024,256]{1,0:T(8,128)(2,1)S(1)}, u32[]{:S(2)}, u32[]{:S(2)}) collective-permute-start(bf16[1024,256]{1,0:T(8,128)(2,1)S(1)} %collective-permute-done.19.refs_19_), channel_id=1, source_target_pairs={{0,1},{1,0},{2,3},{3,2},{4,5},{5,4},{6,7},{7,6},{8,9},{9,8},{10,11... | collective-permute-start | bytes 1572872 | tf_op jit(solution)/shard_map/ppermute | solution.py:37
  113.7 17.5 %collective-permute-start.8 = (bf16[2,1024,256]{2,1,0:T(8,128)(2,1)}, bf16[2,1024,256]{2,1,0:T(8,128)(2,1)S(1)}, u32[]{:S(2)}, u32[]{:S(2)}) collective-permute-start(bf16[2,1024,256]{2,1,0:T(8,128)(2,1)} %collective-permute-done.7.refs_26_), channel_id=1, source_target_pairs={{0,1},{1,0},{2,3},{3,2},{4,5},{5,4},{6,7},{7,6},{8,9},{9,8},{10,11... | collective-permute-start | bytes 3145736 | tf_op jit(solution)/shard_map/ppermute | solution.py:37
  113.8 14.7 %collective-permute-start.21 = (bf16[1024,256]{1,0:T(8,128)(2,1)S(1)}, bf16[1024,256]{1,0:T(8,128)(2,1)}, u32[]{:S(2)}, u32[]{:S(2)}) collective-permute-start(bf16[1024,256]{1,0:T(8,128)(2,1)S(1)} %collective-permute-done.17.refs_18_), channel_id=1, source_target_pairs={{0,2},{1,3},{2,0},{3,1},{4,6},{5,7},{6,4},{7,5},{8,10},{9,11},{10,... | collective-permute-start | bytes 1572872 | tf_op jit(solution)/shard_map/ppermute | solution.py:33
  115.5 15.6 %collective-permute-start.29 = (bf16[2,1024,256]{2,1,0:T(8,128)(2,1)}, bf16[2,1024,256]{2,1,0:T(8,128)(2,1)S(1)}, u32[]{:S(2)}, u32[]{:S(2)}) collective-permute-start(bf16[2,1024,256]{2,1,0:T(8,128)(2,1)} %collective-permute-done.28.refs_29_), channel_id=1, source_target_pairs={{0,64},{1,193},{2,66},{3,195},{4,68},{5,197},{6,70},{7,199},{8,72}... | collective-permute-start | bytes 3145736 | tf_op jit(solution)/shard_map/ppermute | solution.py:46
  115.8 13.9 %collective-permute-start.18 = (bf16[1024,256]{1,0:T(8,128)(2,1)S(1)}, bf16[1024,256]{1,0:T(8,128)(2,1)S(1)}, u32[]{:S(2)}, u32[]{:S(2)}) collective-permute-start(bf16[1024,256]{1,0:T(8,128)(2,1)S(1)} %collective-permute-done.17.refs_18_), channel_id=1, source_target_pairs={{0,1},{1,0},{2,3},{3,2},{4,5},{5,4},{6,7},{7,6},{8,9},{9,8},{10,11... | collective-permute-start | bytes 1572872 | tf_op jit(solution)/shard_map/ppermute | solution.py:37
  119.9 12.4 %collective-permute-start.14 = (bf16[2,1024,256]{2,1,0:T(8,128)(2,1)}, bf16[2,1024,256]{2,1,0:T(8,128)(2,1)}, u32[]{:S(2)}, u32[]{:S(2)}) collective-permute-start(bf16[2,1024,256]{2,1,0:T(8,128)(2,1)} %collective-permute-done.13.refs_23_), channel_id=1, source_target_pairs={{0,1},{1,0},{2,3},{3,2},{4,5},{5,4},{6,7},{7,6},{8,9},{9,8},{10,11... | collective-permute-start | bytes 3145736 | tf_op jit(solution)/shard_map/ppermute | solution.py:37
  128.5 3.1 %collective-permute-start.26 = (bf16[1024,256]{1,0:T(8,128)(2,1)}, bf16[1024,256]{1,0:T(8,128)(2,1)}, u32[]{:S(2)}, u32[]{:S(2)}) collective-permute-start(bf16[1024,256]{1,0:T(8,128)(2,1)} %collective-permute-done.25.refs_15_), channel_id=1, source_target_pairs={{0,1},{1,0},{2,3},{3,2},{4,5},{5,4},{6,7},{7,6},{8,9},{9,8},{10,11... | collective-permute-start | bytes 1572872 | tf_op jit(solution)/shard_map/ppermute | solution.py:37
  129.7 2.6 %collective-permute-start.22 = (bf16[1024,256]{1,0:T(8,128)(2,1)}, bf16[1024,256]{1,0:T(8,128)(2,1)}, u32[]{:S(2)}, u32[]{:S(2)}) collective-permute-start(bf16[1024,256]{1,0:T(8,128)(2,1)} %collective-permute-done.21.refs_20_), channel_id=1, source_target_pairs={{0,1},{1,0},{2,3},{3,2},{4,5},{5,4},{6,7},{7,6},{8,9},{9,8},{10,11... | collective-permute-start | bytes 1572872 | tf_op jit(solution)/shard_map/ppermute | solution.py:37
  (19 other events, 447.9 us)

commit v2 on v1

--- a/solution.py
+++ b/solution.py
@@ -50,35 +50,30 @@
     return lax.ppermute(v, "row", [(r, r ^ 1) for r in range(8)])
 
 
-def mask_kernel(mask, values, out, *apart):
+def mask_kernel(mask, values, *outs):
     for i in range(8):
         for j in range(2):
             at = (slice(i * BLOCK, (i + 1) * BLOCK), slice(j * BLOCK, (j + 1) * BLOCK))
-            if not apart:
-                out[at] = values[at] * mask[j, i].astype(jnp.bfloat16)
-            for d, copy in enumerate(apart):
-                block = values[(d, *at)] * mask[d, j, i].astype(jnp.bfloat16)
-                out[(d, *at)] = block
-                copy[at] = block
+            if len(outs) == 1:
+                outs[0][at] = values[at] * mask[j, i].astype(jnp.bfloat16)
+            else:
+                for d, out in enumerate(outs):
+                    out[at] = values[(d, *at)] * mask[d, j, i].astype(jnp.bfloat16)
 
 
 def masked(values, mask):
-    out = [jax.ShapeDtypeStruct(values.shape, values.dtype)]
-    if len(values.shape) == 3:
-        out += [jax.ShapeDtypeStruct(values.shape[1:], values.dtype)] * values.shape[0]
+    n = 1 if len(values.shape) == 2 else values.shape[0]
+    vmem = pl.BlockSpec(memory_space=pltpu.VMEM)
     return pl.pallas_call(
         mask_kernel,
-        out_shape=out,
-        in_specs=[
-            pl.BlockSpec(memory_space=pltpu.SMEM),
-            pl.BlockSpec(memory_space=pltpu.VMEM),
-        ],
-        out_specs=[pl.BlockSpec(memory_space=pltpu.VMEM)] * len(out),
+        out_shape=[jax.ShapeDtypeStruct(values.shape[-2:], values.dtype)] * n,
+        in_specs=[pl.BlockSpec(memory_space=pltpu.SMEM), vmem],
+        out_specs=[vmem] * n,
         cost_estimate=pl.CostEstimate(flops=10**6, bytes_accessed=2**20, transcendentals=0),
     )(jnp.swapaxes(mask, -1, -2), values)
 
 
-def matmul_kernel(n_a, parts, n_b, pieces, place, keep, *refs):
+def matmul_kernel(parts, n_a, n_b, place, keep, *refs):
     a_refs, refs = refs[:n_a], refs[n_a:]
     b_refs, refs = refs[:n_b], refs[n_b:]
     out, a_vm, b_vm, acc, a_sem, b_sem = refs
@@ -93,35 +88,26 @@
         head = 1 - core if 1 <= delta <= 3 else core
         for j, (which, index) in enumerate(parts[u]):
             ref = a_refs[which] if index is None else a_refs[which].at[index]
-            to = a_vm.at[u, (head + j) % 2]
-            pltpu.make_async_copy(ref, to, a_sem.at[u]).start()
+            pltpu.make_async_copy(ref, a_vm.at[u, (head + j) % 2], a_sem.at[u]).start()
         owner = (z + delta * way + NZ) % NZ
         hops = ((y - owner // 2) * way + NY) % NY
         side = (owner % 2 + lo) % 2
         rows = pl.ds(pl.multiple_of(((hi + far) % 2) * UNIT, UNIT), UNIT)
-        for i in range(4):
-            for low in range(2):
-
-                @pl.when(jnp.logical_and(hops == i, side == low))
-                def _():
-                    for which, d, at, where in pieces:
-                        if (at, where) == (i, low):
-                            if d is None:
-                                source, target = b_refs[which].at[:, rows, :], b_vm.at[u]
-                            else:
-                                source, target = b_refs[which].at[rows, :], b_vm.at[u, d]
-                            pltpu.make_async_copy(source, target, b_sem.at[u]).start()
-
-    def wait(u):
-        pltpu.make_async_copy(b_vm.at[u], b_vm.at[u], b_sem.at[u]).wait()
-        pltpu.make_async_copy(a_vm.at[u], a_vm.at[u], a_sem.at[u]).wait()
+        for n in range(n_b // 2):
+
+            @pl.when(jnp.logical_and(hops == n // 2, side == n % 2))
+            def _():
+                for d in range(2):
+                    source = b_refs[2 * n + d].at[rows, :]
+                    pltpu.make_async_copy(source, b_vm.at[u, d], b_sem.at[u]).start()
 
     for u in range(AHEAD):
         start(u)
     for u in range(n_units):
         if u + AHEAD < n_units:
             start(u + AHEAD)
-        wait(u)
+        pltpu.make_async_copy(b_vm.at[u], b_vm.at[u], b_sem.at[u]).wait()
+        pltpu.make_async_copy(a_vm.at[u], a_vm.at[u], a_sem.at[u]).wait()
         for d in range(2):
             part = sum(
                 jnp.dot(
@@ -152,15 +138,14 @@
     return len(arrays) - 1
 
 
-def multiply(place, keep, units, b_parts):
-    a_arrays, b_arrays = [], []
+def multiply(place, keep, units, b_arrays):
+    a_arrays = []
     parts = [[(listed(a_arrays, v), index) for v, index in unit] for unit in units]
-    pieces = [(listed(b_arrays, v), d, hops, low) for v, d, hops, low in b_parts]
-    n_a, n_b = len(a_arrays), len(b_arrays)
     anywhere = pl.BlockSpec(memory_space=pl.ANY)
     scalars = pl.BlockSpec(memory_space=pltpu.SMEM)
+    n_a, n_b = len(a_arrays), len(b_arrays)
     return pl.pallas_call(
-        functools.partial(matmul_kernel, n_a, parts, n_b, pieces),
+        functools.partial(matmul_kernel, parts, n_a, n_b),
         out_shape=jax.ShapeDtypeStruct((2, ROWS, COLS), jnp.bfloat16),
         in_specs=[scalars, scalars] + [anywhere] * (n_a + n_b),
         out_specs=pl.BlockSpec(memory_space=pltpu.VMEM),
@@ -181,7 +166,7 @@
 def work(density, density_mask, response, response_mask, filter_mask):
     place = jnp.stack([lax.axis_index("row"), lax.axis_index("col")]).astype(jnp.int32)
     (own,) = masked(density, density_mask)
-    b0, b0a, b0b = masked(response, response_mask)
+    b0a, b0b = masked(response, response_mask)
 
     p0o, across = other_core(own), across_x(own)
     q0 = jnp.stack([across, other_core(across)])
@@ -201,12 +186,12 @@
     q4 = along_z(q3a)
     q4o = other_core(q4)
 
-    r1 = along_y(b0)
-    r2 = along_y(r1)
-    r3 = along_y(r2)
+    r1a, r1b = along_y(b0a), along_y(b0b)
+    r2a, r2b = along_y(r1a), along_y(r1b)
+    r3a, r3b = along_y(r2a), along_y(r2b)
     s0a, s0b = beside_x(b0a), beside_x(b0b)
     s1a, s1b = along_y(s0a), along_y(s0b)
-    s2a, s2b = along_y(s1a), along_y(s1b)
+    s2a, s2b = along_y(s1a), beside_x(r2b)
     s3a, s3b = along_y(s2a), along_y(s2b)
 
     both = lambda v: [(v, 0), (v, 1)]
@@ -221,10 +206,8 @@
         two(p2a, p2b), both(q2),
         two(p1a, p1b), both(q1),
     ]
-    b_parts = [(v, None, i, 0) for i, v in enumerate([b0, r1, r2, r3])]
-    for i, pair in enumerate([(s0a, s0b), (s1a, s1b), (s2a, s2b), (s3a, s3b)]):
-        b_parts += [(v, d, i, 1) for d, v in enumerate(pair)]
-    return multiply(place, jnp.swapaxes(filter_mask, 0, 1), units, b_parts)
+    b_arrays = [b0a, b0b, s0a, s0b, r1a, r1b, s1a, s1b, r2a, r2b, s2a, s2b, r3a, r3b, s3a, s3b]
+    return multiply(place, jnp.swapaxes(filter_mask, 0, 1), units, b_arrays)
 
 
 def solution(mesh):

time: 148 us -> 150 us (1.014); the launches traced: 146 us -> 150 us
  waiting for transfers between devices: 68.3 us -> 78.3 us
  starting transfers between devices: 57.6 us -> 52.8 us
    ppermute x9 -> x11, waiting for transfers between devices: 24.7 us -> 38.4 us  [along_y(): return lax.ppermute(v, ('row', 'col'), pairs)]
    ppermute x10, waiting for transfers between devices: 11.2 us -> 0.03 us  [along_z(): lax.ppermute(v, 'col', col_pairs(lambda z, hi, core: (z + 1 - 2 * core, h...]
    ppermute x14, starting transfers between devices: 18.8 us -> 7.92 us  [other_core(): lax.ppermute(v, 'col', col_pairs(lambda z, hi, core: (z, hi, core + 1)))]
    ppermute x3, waiting for transfers between devices: 14 us -> 21.7 us  [across_x(): lax.ppermute(v, 'col', col_pairs(lambda z, hi, core: (z, hi + 1, core)))]
    ppermute x10, starting transfers between devices: 20.6 us -> 23.8 us  [along_z(): lax.ppermute(v, 'col', col_pairs(lambda z, hi, core: (z + 1 - 2 * core, h...]
    ppermute x2 -> x3, starting transfers between devices: 1.47 us -> 3.54 us  [beside_x(): return lax.ppermute(v, 'row', [(r, r ^ 1) for r in range(8)])]
    ppermute x9 -> x11, starting transfers between devices: 10.6 us -> 11.4 us  [along_y(): return lax.ppermute(v, ('row', 'col'), pairs)]
    ppermute x2 -> x3, waiting for transfers between devices: 17.2 us -> 17 us  [beside_x(): return lax.ppermute(v, 'row', [(r, r ^ 1) for r in range(8)])]
  transfers between devices with their start and end apart: 38 -> 41, of which waited for: 15 -> 15; matrix products, arithmetic and copies ran while one was open for 0% -> 0% of each run, Pallas kernels for 2% -> 2%
where the time goes in v2:
time: 150 us
  waiting for transfers between devices  78.3 us (52%)
  starting transfers between devices  52.8 us (35%)
  Pallas kernels  17.8 us (12%)
    ppermute x11, waiting for transfers between devices, along_y(): return lax.ppermute(v, ('row', 'col'), pairs)  38.4 us
    ppermute x10, starting transfers between devices, along_z(): lax.ppermute(v, 'col', col_pairs(lambda z, hi, core: (z + 1 - 2 * core, h...  23.8 us
    ppermute x3, waiting for transfers between devices, across_x(): lax.ppermute(v, 'col', col_pairs(lambda z, hi, core: (z, hi + 1, core)))  21.7 us
    ppermute x3, waiting for transfers between devices, beside_x(): return lax.ppermute(v, 'row', [(r, r ^ 1) for r in range(8)])  17 us
    pallas_call x1, Pallas kernels, multiply(): pl.pallas_call(functools.partial(matmul_kernel, parts, n_a, n_b), out_sha...  13.3 us
    ppermute x11, starting transfers between devices, along_y(): return lax.ppermute(v, ('row', 'col'), pairs)  11.4 us
    ppermute x14, starting transfers between devices, other_core(): lax.ppermute(v, 'col', col_pairs(lambda z, hi, core: (z, hi, core + 1)))  7.92 us
    ppermute x3, starting transfers between devices, across_x(): lax.ppermute(v, 'col', col_pairs(lambda z, hi, core: (z, hi + 1, core)))  6.21 us
  transfers between devices with their start and end apart: 41, of which 15 were waited for; matrix products, arithmetic and copies ran while one was open for 0% of the time, Pallas kernels for 2%

profile of v2, /device:TPU:1, one launch (start us, length us, event | category | flops | bytes accessed | tf_op | source)
XLA Modules:
  0.0 150.1 jit_solution(3881849087766590420)
XLA Ops:
  0.0 2.0 %shard_map.55.refs_0_ = bf16[1024,256]{1,0:T(8,128)(2,1)} custom-call(s32[2,8]{1,0:T(2,128)} %bitcast.10, bf16[1024,256]{1,0:T(8,128)(2,1)} %values.2), custom_call_target="tpu_custom_call" | custom-call | flops 1000000 | bytes 1048576 | tf_op jit(solution)/shard_map/pallas_call | solution.py:67
  2.0 6.4 %collective-permute-start.3 = (bf16[1024,256]{1,0:T(8,128)(2,1)}, bf16[1024,256]{1,0:T(8,128)(2,1)S(1)}, u32[]{:S(2)}, u32[]{:S(2)}) collective-permute-start(bf16[1024,256]{1,0:T(8,128)(2,1)} %shard_map.55.refs_0_), channel_id=1, source_target_pairs={{0,4},{1,29},{2,6},{3,31},{4,8},{5,1},{6,10},{7,3},{8,12},{9,5},{1... | collective-permute-start | bytes 1572872 | tf_op jit(solution)/shard_map/ppermute | solution.py:29
  8.4 2.7 %collective-permute-start.1 = (bf16[1024,256]{1,0:T(8,128)(2,1)}, bf16[1024,256]{1,0:T(8,128)(2,1)S(1)}, u32[]{:S(2)}, u32[]{:S(2)}) collective-permute-start(bf16[1024,256]{1,0:T(8,128)(2,1)} %shard_map.55.refs_0_), channel_id=1, source_target_pairs={{0,2},{1,3},{2,0},{3,1},{4,6},{5,7},{6,4},{7,5},{8,10},{9,11},{10,... | collective-permute-start | bytes 1572872 | tf_op jit(solution)/shard_map/ppermute | solution.py:33
  11.1 2.5 %shard_map.56 = (bf16[1024,256]{1,0:T(8,128)(2,1)}, bf16[1024,256]{1,0:T(8,128)(2,1)}) custom-call(s32[2,2,8]{2,1,0:T(2,128)} %bitcast.9, bf16[2,1024,256]{2,1,0:T(8,128)(2,1)} %values.3), custom_call_target="tpu_custom_call" | custom-call | flops 1000000 | bytes 1048576 | tf_op jit(solution)/shard_map/pallas_call | solution.py:67
  13.6 2.7 %collective-permute-start.29 = (bf16[1024,256]{1,0:T(8,128)(2,1)}, bf16[1024,256]{1,0:T(8,128)(2,1)S(1)}, u32[]{:S(2)}, u32[]{:S(2)}) collective-permute-start(bf16[1024,256]{1,0:T(8,128)(2,1)} %get-tuple-element.7.refs_27_), channel_id=1, source_target_pairs={{0,64},{1,193},{2,66},{3,195},{4,68},{5,197},{6,70},{7,199},{8,72}... | collective-permute-start | bytes 1572872 | tf_op jit(solution)/shard_map/ppermute | solution.py:46
  16.3 0.3 collective-permute-start.27
  16.6 0.9 collective-permute-start.30
  17.6 5.6 %collective-permute-done.1 = bf16[1024,256]{1,0:T(8,128)(2,1)S(1)} collective-permute-done((bf16[1024,256]{1,0:T(8,128)(2,1)}, bf16[1024,256]{1,0:T(8,128)(2,1)S(1)}, u32[]{:S(2)}, u32[]{:S(2)}) %collective-permute-start.1) | collective-permute-done | bytes 524320 | tf_op jit(solution)/shard_map/ppermute | solution.py:33
  23.2 2.1 %collective-permute-start.28 = (bf16[1024,256]{1,0:T(8,128)(2,1)}, bf16[1024,256]{1,0:T(8,128)(2,1)S(1)}, u32[]{:S(2)}, u32[]{:S(2)}) collective-permute-start(bf16[1024,256]{1,0:T(8,128)(2,1)} %get-tuple-element.8.refs_28_), channel_id=1, source_target_pairs={{0,32},{32,0},{64,96},{96,64},{128,160},{160,128},{192,224},{224,1... | collective-permute-start | bytes 1572872 | tf_op jit(solution)/shard_map/ppermute | solution.py:50
  25.2 0.3 collective-permute-start.9
  25.6 9.8 %collective-permute-done.27.refs_29_ = bf16[1024,256]{1,0:T(8,128)(2,1)S(1)} collective-permute-done((bf16[1024,256]{1,0:T(8,128)(2,1)}, bf16[1024,256]{1,0:T(8,128)(2,1)S(1)}, u32[]{:S(2)}, u32[]{:S(2)}) %collective-permute-start.27) | collective-permute-done | bytes 524320 | tf_op jit(solution)/shard_map/ppermute | solution.py:50
  35.4 1.5 %collective-permute-start.5 = (bf16[1024,256]{1,0:T(8,128)(2,1)S(1)}, bf16[1024,256]{1,0:T(8,128)(2,1)S(1)}, u32[]{:S(2)}, u32[]{:S(2)}) collective-permute-start(bf16[1024,256]{1,0:T(8,128)(2,1)S(1)} %collective-permute-done.refs_1_), channel_id=1, source_target_pairs={{0,4},{1,29},{2,6},{3,31},{4,8},{5,1},{6,10},{7,3},{8,12},{9,5},{1... | collective-permute-start | bytes 1572872 | tf_op jit(solution)/shard_map/ppermute | solution.py:29
  36.9 7.2 %collective-permute-done.28.refs_30_ = bf16[1024,256]{1,0:T(8,128)(2,1)S(1)} collective-permute-done((bf16[1024,256]{1,0:T(8,128)(2,1)}, bf16[1024,256]{1,0:T(8,128)(2,1)S(1)}, u32[]{:S(2)}, u32[]{:S(2)}) %collective-permute-start.28) | collective-permute-done | bytes 524320 | tf_op jit(solution)/shard_map/ppermute | solution.py:50
  44.1 2.7 %collective-permute-start.33 = (bf16[1024,256]{1,0:T(8,128)(2,1)S(1)}, bf16[1024,256]{1,0:T(8,128)(2,1)S(1)}, u32[]{:S(2)}, u32[]{:S(2)}) collective-permute-start(bf16[1024,256]{1,0:T(8,128)(2,1)S(1)} %collective-permute-done.29.refs_31_), channel_id=1, source_target_pairs={{0,64},{1,193},{2,66},{3,195},{4,68},{5,197},{6,70},{7,199},{8,72}... | collective-permute-start | bytes 1572872 | tf_op jit(solution)/shard_map/ppermute | solution.py:46
  46.8 0.5 collective-permute-start.31
  47.6 2.8 %collective-permute-start.15 = (bf16[1024,256]{1,0:T(8,128)(2,1)S(1)}, bf16[1024,256]{1,0:T(8,128)(2,1)S(1)}, u32[]{:S(2)}, u32[]{:S(2)}) collective-permute-start(bf16[1024,256]{1,0:T(8,128)(2,1)S(1)} %collective-permute-done.9.refs_21_), channel_id=1, source_target_pairs={{0,4},{1,29},{2,6},{3,31},{4,8},{5,1},{6,10},{7,3},{8,12},{9,5},{1... | collective-permute-start | bytes 1572872 | tf_op jit(solution)/shard_map/ppermute | solution.py:29
  50.5 2.5 %collective-permute-done.33.refs_35_ = bf16[1024,256]{1,0:T(8,128)(2,1)S(1)} collective-permute-done((bf16[1024,256]{1,0:T(8,128)(2,1)S(1)}, bf16[1024,256]{1,0:T(8,128)(2,1)S(1)}, u32[]{:S(2)}, u32[]{:S(2)}) %collective-permute-start.33) | collective-permute-done | bytes 524320 | tf_op jit(solution)/shard_map/ppermute | solution.py:46
  52.9 5.6 %collective-permute-done.31.refs_33_ = bf16[1024,256]{1,0:T(8,128)(2,1)S(1)} collective-permute-done((bf16[1024,256]{1,0:T(8,128)(2,1)S(1)}, bf16[1024,256]{1,0:T(8,128)(2,1)S(1)}, u32[]{:S(2)}, u32[]{:S(2)}) %collective-permute-start.31) | collective-permute-done | bytes 524320 | tf_op jit(solution)/shard_map/ppermute | solution.py:46
  58.5 2.8 %collective-permute-start.11 = (bf16[1024,256]{1,0:T(8,128)(2,1)S(1)}, bf16[1024,256]{1,0:T(8,128)(2,1)S(1)}, u32[]{:S(2)}, u32[]{:S(2)}) collective-permute-start(bf16[1024,256]{1,0:T(8,128)(2,1)S(1)} %collective-permute-done.5.refs_25_), channel_id=1, source_target_pairs={{0,4},{1,29},{2,6},{3,31},{4,8},{5,1},{6,10},{7,3},{8,12},{9,5},{1... | collective-permute-start | bytes 1572872 | tf_op jit(solution)/shard_map/ppermute | solution.py:29
  61.4 2.8 %collective-permute-done.34.refs_36_ = bf16[1024,256]{1,0:T(8,128)(2,1)S(1)} collective-permute-done((bf16[1024,256]{1,0:T(8,128)(2,1)S(1)}, bf16[1024,256]{1,0:T(8,128)(2,1)S(1)}, u32[]{:S(2)}, u32[]{:S(2)}) %collective-permute-start.34) | collective-permute-done | bytes 524320 | tf_op jit(solution)/shard_map/ppermute | solution.py:46
  64.4 5.4 %collective-permute-done.32.refs_34_ = bf16[1024,256]{1,0:T(8,128)(2,1)S(1)} collective-permute-done((bf16[1024,256]{1,0:T(8,128)(2,1)S(1)}, bf16[1024,256]{1,0:T(8,128)(2,1)S(1)}, u32[]{:S(2)}, u32[]{:S(2)}) %collective-permute-start.32) | collective-permute-done | bytes 524320 | tf_op jit(solution)/shard_map/ppermute | solution.py:46
  69.8 2.8 %collective-permute-start.7 = (bf16[2,1024,256]{2,1,0:T(8,128)(2,1)S(1)}, bf16[2,1024,256]{2,1,0:T(8,128)(2,1)S(1)}, u32[]{:S(2)}, u32[]{:S(2)}) collective-permute-start(bf16[2,1024,256]{2,1,0:T(8,128)(2,1)S(1)} %pad_maximum_fusion.refs_2_), channel_id=1, source_target_pairs={{0,4},{1,29},{2,6},{3,31},{4,8},{5,1},{6,10},{7,3},{8,12},{9,5},{1... | collective-permute-start | bytes 3145736 | tf_op jit(solution)/shard_map/ppermute | solution.py:29
  72.6 3.2 %collective-permute-start.37 = (bf16[1024,256]{1,0:T(8,128)(2,1)S(1)}, bf16[1024,256]{1,0:T(8,128)(2,1)S(1)}, u32[]{:S(2)}, u32[]{:S(2)}) collective-permute-start(bf16[1024,256]{1,0:T(8,128)(2,1)S(1)} %collective-permute-done.33.refs_35_), channel_id=1, source_target_pairs={{0,64},{1,193},{2,66},{3,195},{4,68},{5,197},{6,70},{7,199},{8,72}... | collective-permute-start | bytes 1572872 | tf_op jit(solution)/shard_map/ppermute | solution.py:46
  76.0 1.2 collective-permute-start.36
  77.2 4.7 %collective-permute-done.37.refs_39_ = bf16[1024,256]{1,0:T(8,128)(2,1)S(1)} collective-permute-done((bf16[1024,256]{1,0:T(8,128)(2,1)S(1)}, bf16[1024,256]{1,0:T(8,128)(2,1)S(1)}, u32[]{:S(2)}, u32[]{:S(2)}) %collective-permute-start.37) | collective-permute-done | bytes 524320 | tf_op jit(solution)/shard_map/ppermute | solution.py:46
  82.0 5.6 %collective-permute-done.35.refs_37_ = bf16[1024,256]{1,0:T(8,128)(2,1)S(1)} collective-permute-done((bf16[1024,256]{1,0:T(8,128)(2,1)S(1)}, bf16[1024,256]{1,0:T(8,128)(2,1)S(1)}, u32[]{:S(2)}, u32[]{:S(2)}) %collective-permute-start.35) | collective-permute-done | bytes 524320 | tf_op jit(solution)/shard_map/ppermute | solution.py:46
  87.6 1.7 %collective-permute-start.19 = (bf16[1024,256]{1,0:T(8,128)(2,1)S(1)}, bf16[1024,256]{1,0:T(8,128)(2,1)S(1)}, u32[]{:S(2)}, u32[]{:S(2)}) collective-permute-start(bf16[1024,256]{1,0:T(8,128)(2,1)S(1)} %collective-permute-done.15.refs_17_), channel_id=1, source_target_pairs={{0,2},{1,3},{2,0},{3,1},{4,6},{5,7},{6,4},{7,5},{8,10},{9,11},{10,... | collective-permute-start | bytes 1572872 | tf_op jit(solution)/shard_map/ppermute | solution.py:33
  89.3 3.9 %collective-permute-done.38.refs_40_ = bf16[1024,256]{1,0:T(8,128)(2,1)S(1)} collective-permute-done((bf16[1024,256]{1,0:T(8,128)(2,1)S(1)}, bf16[1024,256]{1,0:T(8,128)(2,1)S(1)}, u32[]{:S(2)}, u32[]{:S(2)}) %collective-permute-start.38) | collective-permute-done | bytes 524320 | tf_op jit(solution)/shard_map/ppermute | solution.py:46
  93.2 3.5 %collective-permute-start.17 = (bf16[1024,256]{1,0:T(8,128)(2,1)S(1)}, bf16[1024,256]{1,0:T(8,128)(2,1)}, u32[]{:S(2)}, u32[]{:S(2)}) collective-permute-start(bf16[1024,256]{1,0:T(8,128)(2,1)S(1)} %collective-permute-done.11.refs_22_), channel_id=1, source_target_pairs={{0,4},{1,29},{2,6},{3,31},{4,8},{5,1},{6,10},{7,3},{8,12},{9,5},{1... | collective-permute-start | bytes 1572872 | tf_op jit(solution)/shard_map/ppermute | solution.py:29
  96.7 1.7 %collective-permute-start.13 = (bf16[2,1024,256]{2,1,0:T(8,128)(2,1)S(1)}, bf16[2,1024,256]{2,1,0:T(8,128)(2,1)S(1)}, u32[]{:S(2)}, u32[]{:S(2)}) collective-permute-start(bf16[2,1024,256]{2,1,0:T(8,128)(2,1)S(1)} %collective-permute-done.7.refs_26_), channel_id=1, source_target_pairs={{0,4},{1,29},{2,6},{3,31},{4,8},{5,1},{6,10},{7,3},{8,12},{9,5},{1... | collective-permute-start | bytes 3145736 | tf_op jit(solution)/shard_map/ppermute | solution.py:29
  98.4 3.8 %collective-permute-done.19.refs_19_ = bf16[1024,256]{1,0:T(8,128)(2,1)S(1)} collective-permute-done((bf16[1024,256]{1,0:T(8,128)(2,1)S(1)}, bf16[1024,256]{1,0:T(8,128)(2,1)S(1)}, u32[]{:S(2)}, u32[]{:S(2)}) %collective-permute-start.19) | collective-permute-done | bytes 524320 | tf_op jit(solution)/shard_map/ppermute | solution.py:33
  102.3 0.3 collective-permute-start.39
  102.6 0.5 collective-permute-start.40
  103.1 1.3 collective-permute-start.24
  104.3 1.8 %collective-permute-start.25 = (bf16[1024,256]{1,0:T(8,128)(2,1)S(1)}, bf16[1024,256]{1,0:T(8,128)(2,1)}, u32[]{:S(2)}, u32[]{:S(2)}) collective-permute-start(bf16[1024,256]{1,0:T(8,128)(2,1)S(1)} %collective-permute-done.19.refs_19_), channel_id=1, source_target_pairs={{0,4},{1,29},{2,6},{3,31},{4,8},{5,1},{6,10},{7,3},{8,12},{9,5},{1... | collective-permute-start | bytes 1572872 | tf_op jit(solution)/shard_map/ppermute | solution.py:29
  106.1 4.5 %collective-permute-done.39.refs_41_ = bf16[1024,256]{1,0:T(8,128)(2,1)S(1)} collective-permute-done((bf16[1024,256]{1,0:T(8,128)(2,1)S(1)}, bf16[1024,256]{1,0:T(8,128)(2,1)S(1)}, u32[]{:S(2)}, u32[]{:S(2)}) %collective-permute-start.39) | collective-permute-done | bytes 524320 | tf_op jit(solution)/shard_map/ppermute | solution.py:46
  110.6 2.3 %collective-permute-start.20 = (bf16[1024,256]{1,0:T(8,128)(2,1)S(1)}, bf16[1024,256]{1,0:T(8,128)(2,1)S(1)}, u32[]{:S(2)}, u32[]{:S(2)}) collective-permute-start(bf16[1024,256]{1,0:T(8,128)(2,1)S(1)} %collective-permute-done.19.refs_19_), channel_id=1, source_target_pairs={{0,1},{1,0},{2,3},{3,2},{4,5},{5,4},{6,7},{7,6},{8,9},{9,8},{10,11... | collective-permute-start | bytes 1572872 | tf_op jit(solution)/shard_map/ppermute | solution.py:37
  112.9 3.4 %collective-permute-done.40.refs_42_ = bf16[1024,256]{1,0:T(8,128)(2,1)S(1)} collective-permute-done((bf16[1024,256]{1,0:T(8,128)(2,1)S(1)}, bf16[1024,256]{1,0:T(8,128)(2,1)S(1)}, u32[]{:S(2)}, u32[]{:S(2)}) %collective-permute-start.40) | collective-permute-done | bytes 524320 | tf_op jit(solution)/shard_map/ppermute | solution.py:46
  116.3 2.2 %collective-permute-start.8 = (bf16[2,1024,256]{2,1,0:T(8,128)(2,1)S(1)}, bf16[2,1024,256]{2,1,0:T(8,128)(2,1)}, u32[]{:S(2)}, u32[]{:S(2)}) collective-permute-start(bf16[2,1024,256]{2,1,0:T(8,128)(2,1)S(1)} %collective-permute-done.7.refs_26_), channel_id=1, source_target_pairs={{0,1},{1,0},{2,3},{3,2},{4,5},{5,4},{6,7},{7,6},{8,9},{9,8},{10,11... | collective-permute-start | bytes 3145736 | tf_op jit(solution)/shard_map/ppermute | solution.py:37
  118.6 1.7 %collective-permute-start.21 = (bf16[1024,256]{1,0:T(8,128)(2,1)}, bf16[1024,256]{1,0:T(8,128)(2,1)}, u32[]{:S(2)}, u32[]{:S(2)}) collective-permute-start(bf16[1024,256]{1,0:T(8,128)(2,1)} %collective-permute-done.17.refs_18_), channel_id=1, source_target_pairs={{0,2},{1,3},{2,0},{3,1},{4,6},{5,7},{6,4},{7,5},{8,10},{9,11},{10,... | collective-permute-start | bytes 1572872 | tf_op jit(solution)/shard_map/ppermute | solution.py:33
  120.3 0.5 collective-permute-start.14
  120.8 0.4 collective-permute-start.18
  121.2 0.3 collective-permute-start.26
  121.5 12.3 %collective-permute-done.21.refs_20_ = bf16[1024,256]{1,0:T(8,128)(2,1)} collective-permute-done((bf16[1024,256]{1,0:T(8,128)(2,1)}, bf16[1024,256]{1,0:T(8,128)(2,1)}, u32[]{:S(2)}, u32[]{:S(2)}) %collective-permute-start.21) | collective-permute-done | bytes 524320 | tf_op jit(solution)/shard_map/ppermute | solution.py:33
  133.8 1.0 collective-permute-start.22
  134.8 0.6 pad_add_fusion.place
  135.4 1.2 collective-permute-done.22.refs_12_
  136.6 13.3 %shard_map.57 = bf16[2,1024,256]{2,1,0:T(8,128)(2,1)} custom-call(s32[2]{0:T(128)} %pad_add_fusion.place, s32[2,8]{1,0:T(2,128)} %bitcast.11, bf16[1024,256]{1,0:T(8,128)(2,1)} %shard_map.55.refs_0_, bf16[1024,256]{1,0:T(8,128)(2,1)} %copy-done.4, bf16[2,1024,256]{2,1,0:T(8,128)(2,1)} %copy-done, bf16[1024,256]{1,0:T(8,128)(2,1)} %copy-done.10, ...), custom_call_target="tpu_custom_call" | custom-call | flops 8589934592 | bytes 26214400 | tf_op jit(solution)/shard_map/pallas_call | solution.py:147
  (103 shorter events, 0.9 us)
Async XLA Ops:
  2.0 14.6 %collective-permute-start.3 = (bf16[1024,256]{1,0:T(8,128)(2,1)}, bf16[1024,256]{1,0:T(8,128)(2,1)S(1)}, u32[]{:S(2)}, u32[]{:S(2)}) collective-permute-start(bf16[1024,256]{1,0:T(8,128)(2,1)} %shard_map.55.refs_0_), channel_id=1, source_target_pairs={{0,4},{1,29},{2,6},{3,31},{4,8},{5,1},{6,10},{7,3},{8,12},{9,5},{1... | collective-permute-start | bytes 1572872 | tf_op jit(solution)/shard_map/ppermute | solution.py:29
  8.4 14.8 %collective-permute-start.1 = (bf16[1024,256]{1,0:T(8,128)(2,1)}, bf16[1024,256]{1,0:T(8,128)(2,1)S(1)}, u32[]{:S(2)}, u32[]{:S(2)}) collective-permute-start(bf16[1024,256]{1,0:T(8,128)(2,1)} %shard_map.55.refs_0_), channel_id=1, source_target_pairs={{0,2},{1,3},{2,0},{3,1},{4,6},{5,7},{6,4},{7,5},{8,10},{9,11},{10,... | collective-permute-start | bytes 1572872 | tf_op jit(solution)/shard_map/ppermute | solution.py:33
  11.1 14.1 %collective-permute-start = (bf16[1024,256]{1,0:T(8,128)(2,1)}, bf16[1024,256]{1,0:T(8,128)(2,1)S(1)}, u32[]{:S(2)}, u32[]{:S(2)}) collective-permute-start(bf16[1024,256]{1,0:T(8,128)(2,1)} %shard_map.55.refs_0_), channel_id=1, source_target_pairs={{0,1},{1,0},{2,3},{3,2},{4,5},{5,4},{6,7},{7,6},{8,9},{9,8},{10,11... | collective-permute-start | bytes 1572872 | tf_op jit(solution)/shard_map/ppermute | solution.py:37
  13.6 12.0 %collective-permute-start.29 = (bf16[1024,256]{1,0:T(8,128)(2,1)}, bf16[1024,256]{1,0:T(8,128)(2,1)S(1)}, u32[]{:S(2)}, u32[]{:S(2)}) collective-permute-start(bf16[1024,256]{1,0:T(8,128)(2,1)} %get-tuple-element.7.refs_27_), channel_id=1, source_target_pairs={{0,64},{1,193},{2,66},{3,195},{4,68},{5,197},{6,70},{7,199},{8,72}... | collective-permute-start | bytes 1572872 | tf_op jit(solution)/shard_map/ppermute | solution.py:46
  16.3 19.0 %collective-permute-start.27 = (bf16[1024,256]{1,0:T(8,128)(2,1)}, bf16[1024,256]{1,0:T(8,128)(2,1)S(1)}, u32[]{:S(2)}, u32[]{:S(2)}) collective-permute-start(bf16[1024,256]{1,0:T(8,128)(2,1)} %get-tuple-element.7.refs_27_), channel_id=1, source_target_pairs={{0,32},{32,0},{64,96},{96,64},{128,160},{160,128},{192,224},{224,1... | collective-permute-start | bytes 1572872 | tf_op jit(solution)/shard_map/ppermute | solution.py:50
  16.6 18.7 %collective-permute-start.30 = (bf16[1024,256]{1,0:T(8,128)(2,1)}, bf16[1024,256]{1,0:T(8,128)(2,1)S(1)}, u32[]{:S(2)}, u32[]{:S(2)}) collective-permute-start(bf16[1024,256]{1,0:T(8,128)(2,1)} %get-tuple-element.8.refs_28_), channel_id=1, source_target_pairs={{0,64},{1,193},{2,66},{3,195},{4,68},{5,197},{6,70},{7,199},{8,72}... | collective-permute-start | bytes 1572872 | tf_op jit(solution)/shard_map/ppermute | solution.py:46
  23.2 20.9 %collective-permute-start.28 = (bf16[1024,256]{1,0:T(8,128)(2,1)}, bf16[1024,256]{1,0:T(8,128)(2,1)S(1)}, u32[]{:S(2)}, u32[]{:S(2)}) collective-permute-start(bf16[1024,256]{1,0:T(8,128)(2,1)} %get-tuple-element.8.refs_28_), channel_id=1, source_target_pairs={{0,32},{32,0},{64,96},{96,64},{128,160},{160,128},{192,224},{224,1... | collective-permute-start | bytes 1572872 | tf_op jit(solution)/shard_map/ppermute | solution.py:50
  25.2 21.6 %collective-permute-start.9 = (bf16[1024,256]{1,0:T(8,128)(2,1)S(1)}, bf16[1024,256]{1,0:T(8,128)(2,1)S(1)}, u32[]{:S(2)}, u32[]{:S(2)}) collective-permute-start(bf16[1024,256]{1,0:T(8,128)(2,1)S(1)} %collective-permute-done.3.refs_24_), channel_id=1, source_target_pairs={{0,4},{1,29},{2,6},{3,31},{4,8},{5,1},{6,10},{7,3},{8,12},{9,5},{1... | collective-permute-start | bytes 1572872 | tf_op jit(solution)/shard_map/ppermute | solution.py:29
  25.6 21.7 %collective-permute-start.4 = (bf16[1024,256]{1,0:T(8,128)(2,1)S(1)}, bf16[1024,256]{1,0:T(8,128)(2,1)S(1)}, u32[]{:S(2)}, u32[]{:S(2)}) collective-permute-start(bf16[1024,256]{1,0:T(8,128)(2,1)S(1)} %collective-permute-done.3.refs_24_), channel_id=1, source_target_pairs={{0,1},{1,0},{2,3},{3,2},{4,5},{5,4},{6,7},{7,6},{8,9},{9,8},{10,11... | collective-permute-start | bytes 1572872 | tf_op jit(solution)/shard_map/ppermute | solution.py:37
  35.4 12.1 %collective-permute-start.2 = (bf16[1024,256]{1,0:T(8,128)(2,1)S(1)}, bf16[1024,256]{1,0:T(8,128)(2,1)S(1)}, u32[]{:S(2)}, u32[]{:S(2)}) collective-permute-start(bf16[1024,256]{1,0:T(8,128)(2,1)S(1)} %collective-permute-done.1), channel_id=1, source_target_pairs={{0,1},{1,0},{2,3},{3,2},{4,5},{5,4},{6,7},{7,6},{8,9},{9,8},{10,11... | collective-permute-start | bytes 1572872 | tf_op jit(solution)/shard_map/ppermute | solution.py:37
  35.4 12.2 %collective-permute-start.5 = (bf16[1024,256]{1,0:T(8,128)(2,1)S(1)}, bf16[1024,256]{1,0:T(8,128)(2,1)S(1)}, u32[]{:S(2)}, u32[]{:S(2)}) collective-permute-start(bf16[1024,256]{1,0:T(8,128)(2,1)S(1)} %collective-permute-done.refs_1_), channel_id=1, source_target_pairs={{0,4},{1,29},{2,6},{3,31},{4,8},{5,1},{6,10},{7,3},{8,12},{9,5},{1... | collective-permute-start | bytes 1572872 | tf_op jit(solution)/shard_map/ppermute | solution.py:29
  44.1 8.9 %collective-permute-start.33 = (bf16[1024,256]{1,0:T(8,128)(2,1)S(1)}, bf16[1024,256]{1,0:T(8,128)(2,1)S(1)}, u32[]{:S(2)}, u32[]{:S(2)}) collective-permute-start(bf16[1024,256]{1,0:T(8,128)(2,1)S(1)} %collective-permute-done.29.refs_31_), channel_id=1, source_target_pairs={{0,64},{1,193},{2,66},{3,195},{4,68},{5,197},{6,70},{7,199},{8,72}... | collective-permute-start | bytes 1572872 | tf_op jit(solution)/shard_map/ppermute | solution.py:46
  46.8 11.7 %collective-permute-start.31 = (bf16[1024,256]{1,0:T(8,128)(2,1)S(1)}, bf16[1024,256]{1,0:T(8,128)(2,1)S(1)}, u32[]{:S(2)}, u32[]{:S(2)}) collective-permute-start(bf16[1024,256]{1,0:T(8,128)(2,1)S(1)} %collective-permute-done.27.refs_29_), channel_id=1, source_target_pairs={{0,64},{1,193},{2,66},{3,195},{4,68},{5,197},{6,70},{7,199},{8,72}... | collective-permute-start | bytes 1572872 | tf_op jit(solution)/shard_map/ppermute | solution.py:46
  47.3 16.9 %collective-permute-start.34 = (bf16[1024,256]{1,0:T(8,128)(2,1)S(1)}, bf16[1024,256]{1,0:T(8,128)(2,1)S(1)}, u32[]{:S(2)}, u32[]{:S(2)}) collective-permute-start(bf16[1024,256]{1,0:T(8,128)(2,1)S(1)} %collective-permute-done.30.refs_32_), channel_id=1, source_target_pairs={{0,64},{1,193},{2,66},{3,195},{4,68},{5,197},{6,70},{7,199},{8,72}... | collective-permute-start | bytes 1572872 | tf_op jit(solution)/shard_map/ppermute | solution.py:46
  47.4 22.3 %collective-permute-start.32 = (bf16[1024,256]{1,0:T(8,128)(2,1)S(1)}, bf16[1024,256]{1,0:T(8,128)(2,1)S(1)}, u32[]{:S(2)}, u32[]{:S(2)}) collective-permute-start(bf16[1024,256]{1,0:T(8,128)(2,1)S(1)} %collective-permute-done.28.refs_30_), channel_id=1, source_target_pairs={{0,64},{1,193},{2,66},{3,195},{4,68},{5,197},{6,70},{7,199},{8,72}... | collective-permute-start | bytes 1572872 | tf_op jit(solution)/shard_map/ppermute | solution.py:46
  47.6 25.0 %collective-permute-start.15 = (bf16[1024,256]{1,0:T(8,128)(2,1)S(1)}, bf16[1024,256]{1,0:T(8,128)(2,1)S(1)}, u32[]{:S(2)}, u32[]{:S(2)}) collective-permute-start(bf16[1024,256]{1,0:T(8,128)(2,1)S(1)} %collective-permute-done.9.refs_21_), channel_id=1, source_target_pairs={{0,4},{1,29},{2,6},{3,31},{4,8},{5,1},{6,10},{7,3},{8,12},{9,5},{1... | collective-permute-start | bytes 1572872 | tf_op jit(solution)/shard_map/ppermute | solution.py:29
  52.9 22.9 %collective-permute-start.10 = (bf16[1024,256]{1,0:T(8,128)(2,1)S(1)}, bf16[1024,256]{1,0:T(8,128)(2,1)S(1)}, u32[]{:S(2)}, u32[]{:S(2)}) collective-permute-start(bf16[1024,256]{1,0:T(8,128)(2,1)S(1)} %collective-permute-done.9.refs_21_), channel_id=1, source_target_pairs={{0,1},{1,0},{2,3},{3,2},{4,5},{5,4},{6,7},{7,6},{8,9},{9,8},{10,11... | collective-permute-start | bytes 1572872 | tf_op jit(solution)/shard_map/ppermute | solution.py:37
  58.5 61.7 %copy-start.13 = (bf16[1024,256]{1,0:T(8,128)(2,1)}, bf16[1024,256]{1,0:T(8,128)(2,1)S(1)}, u32[]{:S(2)}) copy-start(bf16[1024,256]{1,0:T(8,128)(2,1)S(1)} %collective-permute-done.31.refs_33_) | copy-start | bytes 1572868
  58.5 17.4 %collective-permute-start.11 = (bf16[1024,256]{1,0:T(8,128)(2,1)S(1)}, bf16[1024,256]{1,0:T(8,128)(2,1)S(1)}, u32[]{:S(2)}, u32[]{:S(2)}) collective-permute-start(bf16[1024,256]{1,0:T(8,128)(2,1)S(1)} %collective-permute-done.5.refs_25_), channel_id=1, source_target_pairs={{0,4},{1,29},{2,6},{3,31},{4,8},{5,1},{6,10},{7,3},{8,12},{9,5},{1... | collective-permute-start | bytes 1572872 | tf_op jit(solution)/shard_map/ppermute | solution.py:29
  64.2 56.6 %copy-start.14 = (bf16[1024,256]{1,0:T(8,128)(2,1)}, bf16[1024,256]{1,0:T(8,128)(2,1)S(1)}, u32[]{:S(2)}) copy-start(bf16[1024,256]{1,0:T(8,128)(2,1)S(1)} %collective-permute-done.34.refs_36_) | copy-start | bytes 1572868
  64.2 11.9 %collective-permute-start.6 = (bf16[1024,256]{1,0:T(8,128)(2,1)S(1)}, bf16[1024,256]{1,0:T(8,128)(2,1)S(1)}, u32[]{:S(2)}, u32[]{:S(2)}) collective-permute-start(bf16[1024,256]{1,0:T(8,128)(2,1)S(1)} %collective-permute-done.5.refs_25_), channel_id=1, source_target_pairs={{0,1},{1,0},{2,3},{3,2},{4,5},{5,4},{6,7},{7,6},{8,9},{9,8},{10,11... | collective-permute-start | bytes 1572872 | tf_op jit(solution)/shard_map/ppermute | solution.py:37
  64.4 72.2 %copy-start = (bf16[2,1024,256]{2,1,0:T(8,128)(2,1)}, bf16[2,1024,256]{2,1,0:T(8,128)(2,1)S(1)}, u32[]{:S(2)}) copy-start(bf16[2,1024,256]{2,1,0:T(8,128)(2,1)S(1)} %pad_maximum_fusion.refs_2_) | copy-start | bytes 3145732
  69.8 51.0 %copy-start.15 = (bf16[1024,256]{1,0:T(8,128)(2,1)}, bf16[1024,256]{1,0:T(8,128)(2,1)S(1)}, u32[]{:S(2)}) copy-start(bf16[1024,256]{1,0:T(8,128)(2,1)S(1)} %collective-permute-done.32.refs_34_) | copy-start | bytes 1572868
  69.8 26.9 %collective-permute-start.7 = (bf16[2,1024,256]{2,1,0:T(8,128)(2,1)S(1)}, bf16[2,1024,256]{2,1,0:T(8,128)(2,1)S(1)}, u32[]{:S(2)}, u32[]{:S(2)}) collective-permute-start(bf16[2,1024,256]{2,1,0:T(8,128)(2,1)S(1)} %pad_maximum_fusion.refs_2_), channel_id=1, source_target_pairs={{0,4},{1,29},{2,6},{3,31},{4,8},{5,1},{6,10},{7,3},{8,12},{9,5},{1... | collective-permute-start | bytes 3145736 | tf_op jit(solution)/shard_map/ppermute | solution.py:29
  72.6 48.6 %copy-start.16 = (bf16[1024,256]{1,0:T(8,128)(2,1)}, bf16[1024,256]{1,0:T(8,128)(2,1)S(1)}, u32[]{:S(2)}) copy-start(bf16[1024,256]{1,0:T(8,128)(2,1)S(1)} %collective-permute-done.15.refs_17_) | copy-start | bytes 1572868
  72.6 9.3 %collective-permute-start.37 = (bf16[1024,256]{1,0:T(8,128)(2,1)S(1)}, bf16[1024,256]{1,0:T(8,128)(2,1)S(1)}, u32[]{:S(2)}, u32[]{:S(2)}) collective-permute-start(bf16[1024,256]{1,0:T(8,128)(2,1)S(1)} %collective-permute-done.33.refs_35_), channel_id=1, source_target_pairs={{0,64},{1,193},{2,66},{3,195},{4,68},{5,197},{6,70},{7,199},{8,72}... | collective-permute-start | bytes 1572872 | tf_op jit(solution)/shard_map/ppermute | solution.py:46
  75.8 11.7 %collective-permute-start.35 = (bf16[1024,256]{1,0:T(8,128)(2,1)S(1)}, bf16[1024,256]{1,0:T(8,128)(2,1)S(1)}, u32[]{:S(2)}, u32[]{:S(2)}) collective-permute-start(bf16[1024,256]{1,0:T(8,128)(2,1)S(1)} %collective-permute-done.31.refs_33_), channel_id=1, source_target_pairs={{0,64},{1,193},{2,66},{3,195},{4,68},{5,197},{6,70},{7,199},{8,72}... | collective-permute-start | bytes 1572872 | tf_op jit(solution)/shard_map/ppermute | solution.py:46
  75.9 17.2 %collective-permute-start.38 = (bf16[1024,256]{1,0:T(8,128)(2,1)S(1)}, bf16[1024,256]{1,0:T(8,128)(2,1)S(1)}, u32[]{:S(2)}, u32[]{:S(2)}) collective-permute-start(bf16[1024,256]{1,0:T(8,128)(2,1)S(1)} %collective-permute-done.34.refs_36_), channel_id=1, source_target_pairs={{0,64},{1,193},{2,66},{3,195},{4,68},{5,197},{6,70},{7,199},{8,72}... | collective-permute-start | bytes 1572872 | tf_op jit(solution)/shard_map/ppermute | solution.py:46
  76.0 57.7 %copy-start.19 = (bf16[1024,256]{1,0:T(8,128)(2,1)}, bf16[1024,256]{1,0:T(8,128)(2,1)S(1)}, u32[]{:S(2)}) copy-start(bf16[1024,256]{1,0:T(8,128)(2,1)S(1)} %collective-permute-done.6.refs_4_) | copy-start | bytes 1572868
  76.0 17.1 %collective-permute-start.36 = (bf16[1024,256]{1,0:T(8,128)(2,1)S(1)}, bf16[1024,256]{1,0:T(8,128)(2,1)S(1)}, u32[]{:S(2)}, u32[]{:S(2)}) collective-permute-start(bf16[1024,256]{1,0:T(8,128)(2,1)S(1)} %collective-permute-done.34.refs_36_), channel_id=1, source_target_pairs={{0,32},{32,0},{64,96},{96,64},{128,160},{160,128},{192,224},{224,1... | collective-permute-start | bytes 1572872 | tf_op jit(solution)/shard_map/ppermute | solution.py:50
  81.9 52.8 %copy-start.20 = (bf16[1024,256]{1,0:T(8,128)(2,1)}, bf16[1024,256]{1,0:T(8,128)(2,1)S(1)}, u32[]{:S(2)}) copy-start(bf16[1024,256]{1,0:T(8,128)(2,1)S(1)} %collective-permute-done.37.refs_39_) | copy-start | bytes 1572868
  81.9 16.5 %collective-permute-start.23 = (bf16[1024,256]{1,0:T(8,128)(2,1)S(1)}, bf16[1024,256]{1,0:T(8,128)(2,1)S(1)}, u32[]{:S(2)}, u32[]{:S(2)}) collective-permute-start(bf16[1024,256]{1,0:T(8,128)(2,1)S(1)} %collective-permute-done.15.refs_17_), channel_id=1, source_target_pairs={{0,4},{1,29},{2,6},{3,31},{4,8},{5,1},{6,10},{7,3},{8,12},{9,5},{1... | collective-permute-start | bytes 1572872 | tf_op jit(solution)/shard_map/ppermute | solution.py:29
  87.6 14.7 %collective-permute-start.19 = (bf16[1024,256]{1,0:T(8,128)(2,1)S(1)}, bf16[1024,256]{1,0:T(8,128)(2,1)S(1)}, u32[]{:S(2)}, u32[]{:S(2)}) collective-permute-start(bf16[1024,256]{1,0:T(8,128)(2,1)S(1)} %collective-permute-done.15.refs_17_), channel_id=1, source_target_pairs={{0,2},{1,3},{2,0},{3,1},{4,6},{5,7},{6,4},{7,5},{8,10},{9,11},{10,... | collective-permute-start | bytes 1572872 | tf_op jit(solution)/shard_map/ppermute | solution.py:33
  93.2 9.4 %collective-permute-start.16 = (bf16[1024,256]{1,0:T(8,128)(2,1)S(1)}, bf16[1024,256]{1,0:T(8,128)(2,1)S(1)}, u32[]{:S(2)}, u32[]{:S(2)}) collective-permute-start(bf16[1024,256]{1,0:T(8,128)(2,1)S(1)} %collective-permute-done.15.refs_17_), channel_id=1, source_target_pairs={{0,1},{1,0},{2,3},{3,2},{4,5},{5,4},{6,7},{7,6},{8,9},{9,8},{10,11... | collective-permute-start | bytes 1572872 | tf_op jit(solution)/shard_map/ppermute | solution.py:37
  93.2 9.9 %collective-permute-start.17 = (bf16[1024,256]{1,0:T(8,128)(2,1)S(1)}, bf16[1024,256]{1,0:T(8,128)(2,1)}, u32[]{:S(2)}, u32[]{:S(2)}) collective-permute-start(bf16[1024,256]{1,0:T(8,128)(2,1)S(1)} %collective-permute-done.11.refs_22_), channel_id=1, source_target_pairs={{0,4},{1,29},{2,6},{3,31},{4,8},{5,1},{6,10},{7,3},{8,12},{9,5},{1... | collective-permute-start | bytes 1572872 | tf_op jit(solution)/shard_map/ppermute | solution.py:29
  96.7 23.6 %collective-permute-start.13 = (bf16[2,1024,256]{2,1,0:T(8,128)(2,1)S(1)}, bf16[2,1024,256]{2,1,0:T(8,128)(2,1)S(1)}, u32[]{:S(2)}, u32[]{:S(2)}) collective-permute-start(bf16[2,1024,256]{2,1,0:T(8,128)(2,1)S(1)} %collective-permute-done.7.refs_26_), channel_id=1, source_target_pairs={{0,4},{1,29},{2,6},{3,31},{4,8},{5,1},{6,10},{7,3},{8,12},{9,5},{1... | collective-permute-start | bytes 3145736 | tf_op jit(solution)/shard_map/ppermute | solution.py:29
  98.4 5.9 %collective-permute-start.12 = (bf16[1024,256]{1,0:T(8,128)(2,1)S(1)}, bf16[1024,256]{1,0:T(8,128)(2,1)S(1)}, u32[]{:S(2)}, u32[]{:S(2)}) collective-permute-start(bf16[1024,256]{1,0:T(8,128)(2,1)S(1)} %collective-permute-done.11.refs_22_), channel_id=1, source_target_pairs={{0,1},{1,0},{2,3},{3,2},{4,5},{5,4},{6,7},{7,6},{8,9},{9,8},{10,11... | collective-permute-start | bytes 1572872 | tf_op jit(solution)/shard_map/ppermute | solution.py:37
  102.3 8.3 %collective-permute-start.39 = (bf16[1024,256]{1,0:T(8,128)(2,1)S(1)}, bf16[1024,256]{1,0:T(8,128)(2,1)S(1)}, u32[]{:S(2)}, u32[]{:S(2)}) collective-permute-start(bf16[1024,256]{1,0:T(8,128)(2,1)S(1)} %collective-permute-done.35.refs_37_), channel_id=1, source_target_pairs={{0,64},{1,193},{2,66},{3,195},{4,68},{5,197},{6,70},{7,199},{8,72}... | collective-permute-start | bytes 1572872 | tf_op jit(solution)/shard_map/ppermute | solution.py:46
  102.6 13.7 %collective-permute-start.40 = (bf16[1024,256]{1,0:T(8,128)(2,1)S(1)}, bf16[1024,256]{1,0:T(8,128)(2,1)S(1)}, u32[]{:S(2)}, u32[]{:S(2)}) collective-permute-start(bf16[1024,256]{1,0:T(8,128)(2,1)S(1)} %collective-permute-done.36.refs_38_), channel_id=1, source_target_pairs={{0,64},{1,193},{2,66},{3,195},{4,68},{5,197},{6,70},{7,199},{8,72}... | collective-permute-start | bytes 1572872 | tf_op jit(solution)/shard_map/ppermute | solution.py:46
  103.1 15.5 %collective-permute-start.24 = (bf16[1024,256]{1,0:T(8,128)(2,1)S(1)}, bf16[1024,256]{1,0:T(8,128)(2,1)S(1)}, u32[]{:S(2)}, u32[]{:S(2)}) collective-permute-start(bf16[1024,256]{1,0:T(8,128)(2,1)S(1)} %collective-permute-done.23.refs_13_), channel_id=1, source_target_pairs={{0,1},{1,0},{2,3},{3,2},{4,5},{5,4},{6,7},{7,6},{8,9},{9,8},{10,11... | collective-permute-start | bytes 1572872 | tf_op jit(solution)/shard_map/ppermute | solution.py:37
  104.3 16.4 %collective-permute-start.25 = (bf16[1024,256]{1,0:T(8,128)(2,1)S(1)}, bf16[1024,256]{1,0:T(8,128)(2,1)}, u32[]{:S(2)}, u32[]{:S(2)}) collective-permute-start(bf16[1024,256]{1,0:T(8,128)(2,1)S(1)} %collective-permute-done.19.refs_19_), channel_id=1, source_target_pairs={{0,4},{1,29},{2,6},{3,31},{4,8},{5,1},{6,10},{7,3},{8,12},{9,5},{1... | collective-permute-start | bytes 1572872 | tf_op jit(solution)/shard_map/ppermute | solution.py:29
  110.6 10.6 %collective-permute-start.20 = (bf16[1024,256]{1,0:T(8,128)(2,1)S(1)}, bf16[1024,256]{1,0:T(8,128)(2,1)S(1)}, u32[]{:S(2)}, u32[]{:S(2)}) collective-permute-start(bf16[1024,256]{1,0:T(8,128)(2,1)S(1)} %collective-permute-done.19.refs_19_), channel_id=1, source_target_pairs={{0,1},{1,0},{2,3},{3,2},{4,5},{5,4},{6,7},{7,6},{8,9},{9,8},{10,11... | collective-permute-start | bytes 1572872 | tf_op jit(solution)/shard_map/ppermute | solution.py:37
  116.3 19.1 %collective-permute-start.8 = (bf16[2,1024,256]{2,1,0:T(8,128)(2,1)S(1)}, bf16[2,1024,256]{2,1,0:T(8,128)(2,1)}, u32[]{:S(2)}, u32[]{:S(2)}) collective-permute-start(bf16[2,1024,256]{2,1,0:T(8,128)(2,1)S(1)} %collective-permute-done.7.refs_26_), channel_id=1, source_target_pairs={{0,1},{1,0},{2,3},{3,2},{4,5},{5,4},{6,7},{7,6},{8,9},{9,8},{10,11... | collective-permute-start | bytes 3145736 | tf_op jit(solution)/shard_map/ppermute | solution.py:37
  118.6 15.2 %collective-permute-start.21 = (bf16[1024,256]{1,0:T(8,128)(2,1)}, bf16[1024,256]{1,0:T(8,128)(2,1)}, u32[]{:S(2)}, u32[]{:S(2)}) collective-permute-start(bf16[1024,256]{1,0:T(8,128)(2,1)} %collective-permute-done.17.refs_18_), channel_id=1, source_target_pairs={{0,2},{1,3},{2,0},{3,1},{4,6},{5,7},{6,4},{7,5},{8,10},{9,11},{10,... | collective-permute-start | bytes 1572872 | tf_op jit(solution)/shard_map/ppermute | solution.py:33
  120.3 16.3 %collective-permute-start.14 = (bf16[2,1024,256]{2,1,0:T(8,128)(2,1)S(1)}, bf16[2,1024,256]{2,1,0:T(8,128)(2,1)}, u32[]{:S(2)}, u32[]{:S(2)}) collective-permute-start(bf16[2,1024,256]{2,1,0:T(8,128)(2,1)S(1)} %collective-permute-done.13.refs_23_), channel_id=1, source_target_pairs={{0,1},{1,0},{2,3},{3,2},{4,5},{5,4},{6,7},{7,6},{8,9},{9,8},{10,11... | collective-permute-start | bytes 3145736 | tf_op jit(solution)/shard_map/ppermute | solution.py:37
  120.8 14.6 %collective-permute-start.18 = (bf16[1024,256]{1,0:T(8,128)(2,1)}, bf16[1024,256]{1,0:T(8,128)(2,1)}, u32[]{:S(2)}, u32[]{:S(2)}) collective-permute-start(bf16[1024,256]{1,0:T(8,128)(2,1)} %collective-permute-done.17.refs_18_), channel_id=1, source_target_pairs={{0,1},{1,0},{2,3},{3,2},{4,5},{5,4},{6,7},{7,6},{8,9},{9,8},{10,11... | collective-permute-start | bytes 1572872 | tf_op jit(solution)/shard_map/ppermute | solution.py:37
  121.2 14.2 %collective-permute-start.26 = (bf16[1024,256]{1,0:T(8,128)(2,1)}, bf16[1024,256]{1,0:T(8,128)(2,1)}, u32[]{:S(2)}, u32[]{:S(2)}) collective-permute-start(bf16[1024,256]{1,0:T(8,128)(2,1)} %collective-permute-done.25.refs_15_), channel_id=1, source_target_pairs={{0,1},{1,0},{2,3},{3,2},{4,5},{5,4},{6,7},{7,6},{8,9},{9,8},{10,11... | collective-permute-start | bytes 1572872 | tf_op jit(solution)/shard_map/ppermute | solution.py:37
  133.8 2.8 %collective-permute-start.22 = (bf16[1024,256]{1,0:T(8,128)(2,1)}, bf16[1024,256]{1,0:T(8,128)(2,1)}, u32[]{:S(2)}, u32[]{:S(2)}) collective-permute-start(bf16[1024,256]{1,0:T(8,128)(2,1)} %collective-permute-done.21.refs_20_), channel_id=1, source_target_pairs={{0,1},{1,0},{2,3},{3,2},{4,5},{5,4},{6,7},{7,6},{8,9},{9,8},{10,11... | collective-permute-start | bytes 1572872 | tf_op jit(solution)/shard_map/ppermute | solution.py:37
  (25 other events, 755.1 us)

commit v3 on v2

v3 whole, which is shorter than its diff:
```python
import functools

import jax
import jax.numpy as jnp
from jax import lax
from jax.experimental import pallas as pl
from jax.experimental.pallas import tpu as pltpu
from jax.sharding import PartitionSpec as P


BLOCK = 128
ROWS = 1024
COLS = 256
UNIT = 512
VMEM_LIMIT = 60 * 2**20
AHEAD = 3
EARLY = [0, 2, 14, 4, 12, 6, 10]
LATE = [1, 3, 15, 5, 13, 7, 11, 9, 8]
NZ, NY = 8, 4


def col_pairs(step):
    pairs = []
    for c in range(32):
        z, hi, core = step(c // 4, (c // 2) % 2, c % 2)
        pairs.append((c, (z % NZ) * 4 + (hi % 2) * 2 + core % 2))
    return pairs


def along_z(v):
    return lax.ppermute(v, "col", col_pairs(lambda z, hi, core: (z + 1 - 2 * core, hi, core)))


def across_x(v):
    return lax.ppermute(v, "col", col_pairs(lambda z, hi, core: (z, hi + 1, core)))


def other_core(v):
    return lax.ppermute(v, "col", col_pairs(lambda z, hi, core: (z, hi, core + 1)))


def along_y(v):
    pairs = []
    for r in range(8):
        for c in range(32):
            y = (r // 2 + 1 - 2 * (c % 2)) % NY
            pairs.append((r * 32 + c, (y * 2 + r % 2) * 32 + c))
    return lax.ppermute(v, ("row", "col"), pairs)


def beside_x(v):
    return lax.ppermute(v, "row", [(r, r ^ 1) for r in range(8)])


def mask_kernel(mask, values, *outs):
    for d, out in enumerate(outs):
        for i in range(8):
            for j in range(2):
                at = (slice(i * BLOCK, (i + 1) * BLOCK), slice(j * BLOCK, (j + 1) * BLOCK))
                out[at] = values[(d, *at)] * mask[d, j, i].astype(jnp.bfloat16)


def masked_pair(values, mask):
    vmem = pl.BlockSpec(memory_space=pltpu.VMEM)
    return pl.pallas_call(
        mask_kernel,
        out_shape=[jax.ShapeDtypeStruct(values.shape[1:], values.dtype)] * 2,
        in_specs=[pl.BlockSpec(memory_space=pltpu.SMEM), vmem],
        out_specs=[vmem] * 2,
        cost_estimate=pl.CostEstimate(flops=10**6, bytes_accessed=2**22, transcendentals=0),
    )(jnp.swapaxes(mask, 1, 2), values)


def masked(values, mask):
    shaped = values.reshape(ROWS // BLOCK, BLOCK, COLS // BLOCK, BLOCK)
    scaled = shaped * mask.astype(values.dtype)[:, None, :, None]
    return scaled.reshape(values.shape)


def whereabouts():
    row, col = lax.axis_index("row"), lax.axis_index("col")
    y, lo = row // 2, row % 2
    z, hi, core = col // 4, (col // 2) % 2, col % 2
    return y, lo, z, hi, core, 1 - 2 * core


class Fetch:
    def __init__(self, parts, a_refs, b_refs, a_vm, b_vm, a_sem, b_sem):
        self.y, self.lo, self.z, self.hi, self.core, self.way = whereabouts()
        self.parts, self.a_refs, self.b_refs = parts, a_refs, b_refs
        self.a_vm, self.b_vm, self.a_sem, self.b_sem = a_vm, b_vm, a_sem, b_sem

    def origin(self, u):
        owner = (self.z + (u // 2) * self.way + NZ) % NZ
        hops = ((self.y - owner // 2) * self.way + NY) % NY
        return hops, (owner % 2 + self.lo) % 2

    def start_a(self, u, slot):
        head = 1 - self.core if 1 <= u // 2 <= 3 else self.core
        for j, (which, index) in enumerate(self.parts[u]):
            ref = self.a_refs[which] if index is None else self.a_refs[which].at[index]
            to = self.a_vm.at[slot, (head + j) % 2]
            pltpu.make_async_copy(ref, to, self.a_sem.at[slot]).start()

    def start_b(self, far, hops, side, slot, choices):
        rows = pl.ds(pl.multiple_of(((self.hi + far) % 2) * UNIT, UNIT), UNIT)
        for n in choices:

            @pl.when(jnp.logical_and(hops == n // 2, side == n % 2))
            def _():
                for d in range(2):
                    source = self.b_refs[2 * n + d].at[rows, :]
                    to = self.b_vm.at[slot, d]
                    pltpu.make_async_copy(source, to, self.b_sem.at[slot]).start()

    def start(self, u, slot):
        self.start_a(u, slot)
        self.start_b(u % 2, *self.origin(u), slot, range(len(self.b_refs) // 2))

    def wait(self, slot):
        for vm, sem in ((self.b_vm, self.b_sem), (self.a_vm, self.a_sem)):
            pltpu.make_async_copy(vm.at[slot], vm.at[slot], sem.at[slot]).wait()

    def product(self, slot, d):
        return sum(
            jnp.dot(
                self.a_vm[slot, c],
                self.b_vm[slot, d, c * COLS : (c + 1) * COLS, :],
                preferred_element_type=jnp.float32,
            )
            for c in range(2)
        )


def early_kernel(parts, n_a, n_b, *refs):
    out, a_vm, b_vm, acc, a_sem, b_sem, acc_sem = refs[n_a + n_b :]
    fetch = Fetch(parts, refs[:n_a], refs[n_a : n_a + n_b], a_vm, b_vm, a_sem, b_sem)

    def due(n):
        return fetch.origin(EARLY[n])[0] != 3

    def start(n):
        pl.when(due(n))(lambda: fetch.start(EARLY[n], n))

    def add(n):
        fetch.wait(n)
        for d in range(2):
            acc[d] += fetch.product(n, d)

    for n in range(AHEAD + 1):
        start(n)
    acc[...] = jnp.zeros_like(acc)
    for n in range(len(EARLY)):
        if n + AHEAD + 1 < len(EARLY):
            start(n + AHEAD + 1)
        pl.when(due(n))(functools.partial(add, n))
    store = pltpu.make_async_copy(acc, out, acc_sem)
    store.start()
    store.wait()


def late_kernel(parts, n_a, n_b, *refs):
    before, keep_in, out, a_vm, b_vm, acc, earlier, *refs_left = refs[n_a + n_b :]
    a_sem, b_sem, acc_sem, keep, done, out_sem = refs_left
    fetch = Fetch(parts, refs[:n_a], refs[n_a : n_a + n_b], a_vm, b_vm, a_sem, b_sem)
    n_late = len(LATE)

    owner_y = (fetch.y - 3 * fetch.way + 3 * NY) % NY
    deltas = [((owner_y * 2 + t - fetch.z) * fetch.way + 2 * NZ) % NZ for t in range(2)]

    def start(n):
        if n < n_late:
            fetch.start(LATE[n], n)
            return
        t = n - n_late
        for u in EARLY:
            pl.when(deltas[t] == u // 2)(functools.partial(fetch.start_a, u, n))

        @pl.when(deltas[t] != 4)
        def _():
            fetch.start_b(0, 3, (t + fetch.lo) % 2, n, (6, 7))

    def add(n):
        fetch.wait(n)
        for d in range(2):
            acc[d] += fetch.product(n, d)

    order = [*range(n_late - 1), n_late, n_late + 1, n_late - 1]
    for n in order[:AHEAD]:
        start(n)
    load = pltpu.make_async_copy(before, earlier, acc_sem.at[0])
    keep_load = pltpu.make_async_copy(keep_in, keep, acc_sem.at[1])
    stores = [pltpu.make_async_copy(done.at[d], out.at[d], out_sem.at[d]) for d in range(2)]
    for i, n in enumerate(order):
        if i + AHEAD < len(order):
            start(order[i + AHEAD])
        if i == 0:
            load.start()
            keep_load.start()
            fetch.wait(n)
            for d in range(2):
                acc[d] = fetch.product(n, d)
        elif i < len(order) - 1:
            if n < n_late:
                add(n)
            else:
                pl.when(deltas[n - n_late] != 4)(functools.partial(add, n))
        else:
            fetch.wait(n)
            load.wait()
            keep_load.wait()
            for d in range(2):
                total = acc[d] + earlier[d] + fetch.product(n, d)
                for i in range(8):
                    for j in range(2):
                        scale = keep[j, i].astype(jnp.float32)
                        at = (slice(i * BLOCK, (i + 1) * BLOCK), slice(j * BLOCK, (j + 1) * BLOCK))
                        done[(d, *at)] = (total[at] * scale).astype(jnp.bfloat16)
                stores[d].start()
    for store in stores:
        store.wait()


def listed(arrays, array):
    for n, other in enumerate(arrays):
        if other is array:
            return n
    arrays.append(array)
    return len(arrays) - 1


def multiply(units, b_arrays, before=None, keep=None):
    late = before is not None
    a_arrays, parts = [], {}
    for u, unit in enumerate(units):
        if late or u in EARLY:
            parts[u] = [(listed(a_arrays, v), index) for v, index in unit]
    operands = [*a_arrays, *b_arrays] + ([before, keep] if late else [])
    slots = len(LATE) + 2 if late else len(EARLY)
    total = pltpu.VMEM((2, ROWS, COLS), jnp.float32)
    scratch = [
        pltpu.VMEM((slots, 2, ROWS, COLS), jnp.bfloat16),
        pltpu.VMEM((slots, 2, UNIT, COLS), jnp.bfloat16),
        *[total] * (1 + late),
        pltpu.SemaphoreType.DMA((slots,)),
        pltpu.SemaphoreType.DMA((slots,)),
    ]
    if late:
        scratch += [
            pltpu.SemaphoreType.DMA((2,)),
            pltpu.SMEM(keep.shape, keep.dtype),
            pltpu.VMEM((2, ROWS, COLS), jnp.bfloat16),
            pltpu.SemaphoreType.DMA((2,)),
        ]
    else:
        scratch.append(pltpu.SemaphoreType.DMA)
    kernel = late_kernel if late else early_kernel
    return pl.pallas_call(
        functools.partial(kernel, parts, len(a_arrays), len(b_arrays)),
        out_shape=jax.ShapeDtypeStruct((2, ROWS, COLS), jnp.bfloat16 if late else jnp.float32),
        in_specs=[pl.BlockSpec(memory_space=pl.ANY)] * len(operands),
        out_specs=pl.BlockSpec(memory_space=pl.ANY),
        scratch_shapes=scratch,
        compiler_params=pltpu.CompilerParams(vmem_limit_bytes=VMEM_LIMIT),
        cost_estimate=pl.CostEstimate(
            flops=2 * 2 * ROWS * COLS * UNIT * slots,
            bytes_accessed=slots * 3 * 2**19,
            transcendentals=0,
        ),
    )(*operands)


def work(density, density_mask, response, response_mask, filter_mask):
    own = masked(density, density_mask)
    b0a, b0b = masked_pair(response, response_mask)

    p0o, across = other_core(own), across_x(own)
    q0 = jnp.stack([across, other_core(across)])
    p1a, p1b = along_z(own), along_z(p0o)
    p2a, p2b = along_z(p1a), along_z(p1b)
    p3a, p3b = along_z(p2a), along_z(p2b)
    p1ao, p1bo = other_core(p1a), other_core(p1b)
    p2ao, p2bo = other_core(p2a), other_core(p2b)
    p3ao, p3bo = other_core(p3a), other_core(p3b)
    p4 = along_z(p3a)
    p4o = other_core(p4)
    q3a, q3b = across_x(p3a), across_x(p3b)
    q3ao, q3bo = other_core(q3a), other_core(q3b)
    q1 = along_z(q0)
    q2 = along_z(q1)
    q1o, q2o = other_core(q1), other_core(q2)
    q4 = along_z(q3a)
    q4o = other_core(q4)

    r1a, r1b = along_y(b0a), along_y(b0b)
    r2a, r2b = along_y(r1a), along_y(r1b)
    r3a, r3b = along_y(r2a), along_y(r2b)
    s0a, s0b = beside_x(b0a), beside_x(b0b)
    s1a, s1b = along_y(s0a), along_y(s0b)
    s2a, s2b = along_y(s1a), beside_x(r2b)
    s3a, s3b = along_y(s2a), along_y(s2b)

    both = lambda v: [(v, 0), (v, 1)]
    two = lambda v, w: [(v, None), (w, None)]
    units = [
        two(own, p0o), both(q0),
        two(p1ao, p1bo), both(q1o),
        two(p2ao, p2bo), both(q2o),
        two(p3ao, p3bo), two(q3ao, q3bo),
        two(p4, p4o), two(q4, q4o),
        two(p3a, p3b), two(q3a, q3b),
        two(p2a, p2b), both(q2),
        two(p1a, p1b), both(q1),
    ]
    b_arrays = [b0a, b0b, s0a, s0b, r1a, r1b, s1a, s1b, r2a, r2b, s2a, s2b]
    keep = jnp.swapaxes(filter_mask, 0, 1)
    total = multiply(units, b_arrays)
    return multiply(units, b_arrays + [r3a, r3b, s3a, s3b], total, keep)


def solution(mesh):
    in_specs = (
        P("row", "col"),
        P("row", "col"),
        P(None, "row", "col"),
        P(None, "row", "col"),
        P("row", "col"),
    )
    out_specs = P(None, "row", "col")
    return jax.shard_map(work, mesh=mesh, in_specs=in_specs, out_specs=out_specs, check_vma=False)
```

time: 150 us -> 150 us (level)
  waiting for transfers between devices: 78.3 us -> 72.1 us
  other arithmetic: 0.68 us -> 3.12 us
  local copies, waits for them, and re-layouts: 0.12 us -> 2.12 us
    ppermute x3, waiting for transfers between devices: 21.7 us -> 14.6 us  [across_x(): lax.ppermute(v, 'col', col_pairs(lambda z, hi, core: (z, hi + 1, core)))]
    ppermute x14, starting transfers between devices: 7.92 us -> 10.8 us  [other_core(): lax.ppermute(v, 'col', col_pairs(lambda z, hi, core: (z, hi, core + 1)))]
    ppermute x11, waiting for transfers between devices: 38.4 us -> 40.7 us  [along_y(): return lax.ppermute(v, ('row', 'col'), pairs)]
    ppermute x10, starting transfers between devices: 23.8 us -> 21.5 us  [along_z(): lax.ppermute(v, 'col', col_pairs(lambda z, hi, core: (z + 1 - 2 * core, h...]
    unnamed x64, local copies, waits for them, and re-layouts: 0.12 us -> 1.68 us
  transfers between devices with their start and end apart: 41 -> 41, of which waited for: 15 -> 14; matrix products, arithmetic and copies ran while one was open for 0% -> 1% of each run, Pallas kernels for 2% -> 6%
where the time goes in v3:
time: 150 us
  waiting for transfers between devices  72.1 us (48%)
  starting transfers between devices  53.4 us (36%)
  Pallas kernels  19 us (13%)
  other arithmetic  3.12 us (2%)
  local copies, waits for them, and re-layouts  2.12 us (1%)
    ppermute x11, waiting for transfers between devices, along_y(): return lax.ppermute(v, ('row', 'col'), pairs)  40.7 us
    ppermute x10, starting transfers between devices, along_z(): lax.ppermute(v, 'col', col_pairs(lambda z, hi, core: (z + 1 - 2 * core, h...  21.5 us
    ppermute x3, waiting for transfers between devices, beside_x(): return lax.ppermute(v, 'row', [(r, r ^ 1) for r in range(8)])  16.8 us
    pallas_call x2, Pallas kernels, multiply(): pl.pallas_call(functools.partial(kernel, parts, len(a_arrays), len(b_arra...  16.5 us
    ppermute x3, waiting for transfers between devices, across_x(): lax.ppermute(v, 'col', col_pairs(lambda z, hi, core: (z, hi + 1, core)))  14.6 us
    ppermute x11, starting transfers between devices, along_y(): return lax.ppermute(v, ('row', 'col'), pairs)  11 us
    ppermute x14, starting transfers between devices, other_core(): lax.ppermute(v, 'col', col_pairs(lambda z, hi, core: (z, hi, core + 1)))  10.8 us
    ppermute x3, starting transfers between devices, across_x(): lax.ppermute(v, 'col', col_pairs(lambda z, hi, core: (z, hi + 1, core)))  6.34 us
  transfers between devices with their start and end apart: 41, of which 14 were waited for; matrix products, arithmetic and copies ran while one was open for 1% of the time, Pallas kernels for 6%

profile of v3, /device:TPU:1, one launch (start us, length us, event | category | flops | bytes accessed | tf_op | source)
XLA Modules:
  0.0 150.2 jit_solution(10453217556591724416)
XLA Ops:
  0.0 0.7 convert_element_type.3
  0.8 0.3 mul.11
  1.1 1.1 bitcast_multiply_fusion.refs_0_
  2.3 6.5 %collective-permute-start.3 = (bf16[1024,256]{1,0:T(8,128)(2,1)S(1)}, bf16[1024,256]{1,0:T(8,128)(2,1)S(1)}, u32[]{:S(2)}, u32[]{:S(2)}) collective-permute-start(bf16[1024,256]{1,0:T(8,128)(2,1)S(1)} %bitcast_multiply_fusion.refs_0_), channel_id=1, source_target_pairs={{0,4},{1,29},{2,6},{3,31},{4,8},{5,1},{6,10},{7,3},{8,12},{9,5},{1... | collective-permute-start | bytes 1572872 | tf_op jit(solution)/shard_map/ppermute | solution.py:31
  8.7 2.7 %collective-permute-start.1 = (bf16[1024,256]{1,0:T(8,128)(2,1)S(1)}, bf16[1024,256]{1,0:T(8,128)(2,1)S(1)}, u32[]{:S(2)}, u32[]{:S(2)}) collective-permute-start(bf16[1024,256]{1,0:T(8,128)(2,1)S(1)} %bitcast_multiply_fusion.refs_0_), channel_id=1, source_target_pairs={{0,2},{1,3},{2,0},{3,1},{4,6},{5,7},{6,4},{7,5},{8,10},{9,11},{10,... | collective-permute-start | bytes 1572872 | tf_op jit(solution)/shard_map/ppermute | solution.py:35
  11.5 2.4 %shard_map.55 = (bf16[1024,256]{1,0:T(8,128)(2,1)}, bf16[1024,256]{1,0:T(8,128)(2,1)}) custom-call(s32[2,2,8]{2,1,0:T(2,128)} %bitcast.11, bf16[2,1024,256]{2,1,0:T(8,128)(2,1)} %values.1), custom_call_target="tpu_custom_call" | custom-call | flops 1000000 | bytes 4194304 | tf_op jit(solution)/shard_map/pallas_call | solution.py:65
  13.9 2.7 %collective-permute-start.29 = (bf16[1024,256]{1,0:T(8,128)(2,1)}, bf16[1024,256]{1,0:T(8,128)(2,1)S(1)}, u32[]{:S(2)}, u32[]{:S(2)}) collective-permute-start(bf16[1024,256]{1,0:T(8,128)(2,1)} %get-tuple-element.7.refs_14_.refs_27_), channel_id=1, source_target_pairs={{0,64},{1,193},{2,66},{3,195},{4,68},{5,197},{6,70},{7,199},{8,72}... | collective-permute-start | bytes 1572872 | tf_op jit(solution)/shard_map/ppermute | solution.py:48
  16.6 0.3 collective-permute-start.27
  17.0 0.6 collective-permute-start.30
  17.6 5.6 %collective-permute-done.1 = bf16[1024,256]{1,0:T(8,128)(2,1)S(1)} collective-permute-done((bf16[1024,256]{1,0:T(8,128)(2,1)S(1)}, bf16[1024,256]{1,0:T(8,128)(2,1)S(1)}, u32[]{:S(2)}, u32[]{:S(2)}) %collective-permute-start.1) | collective-permute-done | bytes 524320 | tf_op jit(solution)/shard_map/ppermute | solution.py:35
  23.2 2.2 %collective-permute-start.28 = (bf16[1024,256]{1,0:T(8,128)(2,1)}, bf16[1024,256]{1,0:T(8,128)(2,1)S(1)}, u32[]{:S(2)}, u32[]{:S(2)}) collective-permute-start(bf16[1024,256]{1,0:T(8,128)(2,1)} %get-tuple-element.8.refs_15_.refs_28_), channel_id=1, source_target_pairs={{0,32},{32,0},{64,96},{96,64},{128,160},{160,128},{192,224},{224,1... | collective-permute-start | bytes 1572872 | tf_op jit(solution)/shard_map/ppermute | solution.py:52
  25.4 0.2 collective-permute-start.9
  25.6 9.7 %collective-permute-done.27.refs_16_.refs_29_ = bf16[1024,256]{1,0:T(8,128)(2,1)S(1)} collective-permute-done((bf16[1024,256]{1,0:T(8,128)(2,1)}, bf16[1024,256]{1,0:T(8,128)(2,1)S(1)}, u32[]{:S(2)}, u32[]{:S(2)}) %collective-permute-start.27) | collective-permute-done | bytes 524320 | tf_op jit(solution)/shard_map/ppermute | solution.py:52
  35.4 1.8 %collective-permute-start.5 = (bf16[1024,256]{1,0:T(8,128)(2,1)S(1)}, bf16[1024,256]{1,0:T(8,128)(2,1)S(1)}, u32[]{:S(2)}, u32[]{:S(2)}) collective-permute-start(bf16[1024,256]{1,0:T(8,128)(2,1)S(1)} %collective-permute-done.refs_1_), channel_id=1, source_target_pairs={{0,4},{1,29},{2,6},{3,31},{4,8},{5,1},{6,10},{7,3},{8,12},{9,5},{1... | collective-permute-start | bytes 1572872 | tf_op jit(solution)/shard_map/ppermute | solution.py:31
  37.1 7.1 %collective-permute-done.28.refs_17_.refs_30_ = bf16[1024,256]{1,0:T(8,128)(2,1)S(1)} collective-permute-done((bf16[1024,256]{1,0:T(8,128)(2,1)}, bf16[1024,256]{1,0:T(8,128)(2,1)S(1)}, u32[]{:S(2)}, u32[]{:S(2)}) %collective-permute-start.28) | collective-permute-done | bytes 524320 | tf_op jit(solution)/shard_map/ppermute | solution.py:52
  44.2 2.7 %collective-permute-start.33 = (bf16[1024,256]{1,0:T(8,128)(2,1)S(1)}, bf16[1024,256]{1,0:T(8,128)(2,1)S(1)}, u32[]{:S(2)}, u32[]{:S(2)}) collective-permute-start(bf16[1024,256]{1,0:T(8,128)(2,1)S(1)} %collective-permute-done.29.refs_18_.refs_31_), channel_id=1, source_target_pairs={{0,64},{1,193},{2,66},{3,195},{4,68},{5,197},{6,70},{7,199},{8,72}... | collective-permute-start | bytes 1572872 | tf_op jit(solution)/shard_map/ppermute | solution.py:48
  47.0 0.5 collective-permute-start.31
  47.8 2.7 %collective-permute-start.15 = (bf16[1024,256]{1,0:T(8,128)(2,1)S(1)}, bf16[1024,256]{1,0:T(8,128)(2,1)S(1)}, u32[]{:S(2)}, u32[]{:S(2)}) collective-permute-start(bf16[1024,256]{1,0:T(8,128)(2,1)S(1)} %collective-permute-done.9.refs_10_.refs_21_), channel_id=1, source_target_pairs={{0,4},{1,29},{2,6},{3,31},{4,8},{5,1},{6,10},{7,3},{8,12},{9,5},{1... | collective-permute-start | bytes 1572872 | tf_op jit(solution)/shard_map/ppermute | solution.py:31
  50.5 2.6 %collective-permute-done.33.refs_22_.refs_35_ = bf16[1024,256]{1,0:T(8,128)(2,1)S(1)} collective-permute-done((bf16[1024,256]{1,0:T(8,128)(2,1)S(1)}, bf16[1024,256]{1,0:T(8,128)(2,1)S(1)}, u32[]{:S(2)}, u32[]{:S(2)}) %collective-permute-start.33) | collective-permute-done | bytes 524320 | tf_op jit(solution)/shard_map/ppermute | solution.py:48
  53.1 5.6 %collective-permute-done.31.refs_20_.refs_33_ = bf16[1024,256]{1,0:T(8,128)(2,1)S(1)} collective-permute-done((bf16[1024,256]{1,0:T(8,128)(2,1)S(1)}, bf16[1024,256]{1,0:T(8,128)(2,1)S(1)}, u32[]{:S(2)}, u32[]{:S(2)}) %collective-permute-start.31) | collective-permute-done | bytes 524320 | tf_op jit(solution)/shard_map/ppermute | solution.py:48
  58.7 2.7 %collective-permute-start.11 = (bf16[1024,256]{1,0:T(8,128)(2,1)S(1)}, bf16[1024,256]{1,0:T(8,128)(2,1)S(1)}, u32[]{:S(2)}, u32[]{:S(2)}) collective-permute-start(bf16[1024,256]{1,0:T(8,128)(2,1)S(1)} %collective-permute-done.5.refs_13_.refs_25_), channel_id=1, source_target_pairs={{0,4},{1,29},{2,6},{3,31},{4,8},{5,1},{6,10},{7,3},{8,12},{9,5},{1... | collective-permute-start | bytes 1572872 | tf_op jit(solution)/shard_map/ppermute | solution.py:31
  61.4 2.9 %collective-permute-done.34.refs_23_.refs_36_ = bf16[1024,256]{1,0:T(8,128)(2,1)S(1)} collective-permute-done((bf16[1024,256]{1,0:T(8,128)(2,1)S(1)}, bf16[1024,256]{1,0:T(8,128)(2,1)S(1)}, u32[]{:S(2)}, u32[]{:S(2)}) %collective-permute-start.34) | collective-permute-done | bytes 524320 | tf_op jit(solution)/shard_map/ppermute | solution.py:48
  64.3 1.3 pad_maximum_fusion.refs_2_
  65.7 4.3 %collective-permute-done.32.refs_21_.refs_34_ = bf16[1024,256]{1,0:T(8,128)(2,1)S(1)} collective-permute-done((bf16[1024,256]{1,0:T(8,128)(2,1)S(1)}, bf16[1024,256]{1,0:T(8,128)(2,1)S(1)}, u32[]{:S(2)}, u32[]{:S(2)}) %collective-permute-start.32) | collective-permute-done | bytes 524320 | tf_op jit(solution)/shard_map/ppermute | solution.py:48
  69.9 2.7 %collective-permute-start.7 = (bf16[2,1024,256]{2,1,0:T(8,128)(2,1)S(1)}, bf16[2,1024,256]{2,1,0:T(8,128)(2,1)}, u32[]{:S(2)}, u32[]{:S(2)}) collective-permute-start(bf16[2,1024,256]{2,1,0:T(8,128)(2,1)S(1)} %pad_maximum_fusion.refs_2_), channel_id=1, source_target_pairs={{0,4},{1,29},{2,6},{3,31},{4,8},{5,1},{6,10},{7,3},{8,12},{9,5},{1... | collective-permute-start | bytes 3145736 | tf_op jit(solution)/shard_map/ppermute | solution.py:31
  72.7 3.1 %collective-permute-start.37 = (bf16[1024,256]{1,0:T(8,128)(2,1)S(1)}, bf16[1024,256]{1,0:T(8,128)(2,1)S(1)}, u32[]{:S(2)}, u32[]{:S(2)}) collective-permute-start(bf16[1024,256]{1,0:T(8,128)(2,1)S(1)} %collective-permute-done.33.refs_22_.refs_35_), channel_id=1, source_target_pairs={{0,64},{1,193},{2,66},{3,195},{4,68},{5,197},{6,70},{7,199},{8,72}... | collective-permute-start | bytes 1572872 | tf_op jit(solution)/shard_map/ppermute | solution.py:48
  76.0 1.2 collective-permute-start.36
  77.2 4.7 %collective-permute-done.37.refs_39_ = bf16[1024,256]{1,0:T(8,128)(2,1)S(1)} collective-permute-done((bf16[1024,256]{1,0:T(8,128)(2,1)S(1)}, bf16[1024,256]{1,0:T(8,128)(2,1)S(1)}, u32[]{:S(2)}, u32[]{:S(2)}) %collective-permute-start.37) | collective-permute-done | bytes 524320 | tf_op jit(solution)/shard_map/ppermute | solution.py:48
  82.0 5.5 %collective-permute-done.35.refs_24_.refs_37_ = bf16[1024,256]{1,0:T(8,128)(2,1)S(1)} collective-permute-done((bf16[1024,256]{1,0:T(8,128)(2,1)S(1)}, bf16[1024,256]{1,0:T(8,128)(2,1)S(1)}, u32[]{:S(2)}, u32[]{:S(2)}) %collective-permute-start.35) | collective-permute-done | bytes 524320 | tf_op jit(solution)/shard_map/ppermute | solution.py:48
  87.5 1.7 %collective-permute-start.19 = (bf16[1024,256]{1,0:T(8,128)(2,1)S(1)}, bf16[1024,256]{1,0:T(8,128)(2,1)}, u32[]{:S(2)}, u32[]{:S(2)}) collective-permute-start(bf16[1024,256]{1,0:T(8,128)(2,1)S(1)} %collective-permute-done.15.refs_8_.refs_17_), channel_id=1, source_target_pairs={{0,2},{1,3},{2,0},{3,1},{4,6},{5,7},{6,4},{7,5},{8,10},{9,11},{10,... | collective-permute-start | bytes 1572872 | tf_op jit(solution)/shard_map/ppermute | solution.py:35
  89.3 3.9 %collective-permute-done.38.refs_40_ = bf16[1024,256]{1,0:T(8,128)(2,1)S(1)} collective-permute-done((bf16[1024,256]{1,0:T(8,128)(2,1)S(1)}, bf16[1024,256]{1,0:T(8,128)(2,1)S(1)}, u32[]{:S(2)}, u32[]{:S(2)}) %collective-permute-start.38) | collective-permute-done | bytes 524320 | tf_op jit(solution)/shard_map/ppermute | solution.py:48
  93.2 0.8 copy-done.26
  93.9 3.0 %collective-permute-start.17 = (bf16[1024,256]{1,0:T(8,128)(2,1)S(1)}, bf16[1024,256]{1,0:T(8,128)(2,1)S(1)}, u32[]{:S(2)}, u32[]{:S(2)}) collective-permute-start(bf16[1024,256]{1,0:T(8,128)(2,1)S(1)} %collective-permute-done.11.refs_11_.refs_22_), channel_id=1, source_target_pairs={{0,4},{1,29},{2,6},{3,31},{4,8},{5,1},{6,10},{7,3},{8,12},{9,5},{1... | collective-permute-start | bytes 1572872 | tf_op jit(solution)/shard_map/ppermute | solution.py:31
  96.9 1.7 %collective-permute-start.13 = (bf16[2,1024,256]{2,1,0:T(8,128)(2,1)}, bf16[2,1024,256]{2,1,0:T(8,128)(2,1)}, u32[]{:S(2)}, u32[]{:S(2)}) collective-permute-start(bf16[2,1024,256]{2,1,0:T(8,128)(2,1)} %collective-permute-done.7.refs_26_), channel_id=1, source_target_pairs={{0,4},{1,29},{2,6},{3,31},{4,8},{5,1},{6,10},{7,3},{8,12},{9,5},{1... | collective-permute-start | bytes 3145736 | tf_op jit(solution)/shard_map/ppermute | solution.py:31
  98.7 3.9 %collective-permute-done.19.refs_19_ = bf16[1024,256]{1,0:T(8,128)(2,1)} collective-permute-done((bf16[1024,256]{1,0:T(8,128)(2,1)S(1)}, bf16[1024,256]{1,0:T(8,128)(2,1)}, u32[]{:S(2)}, u32[]{:S(2)}) %collective-permute-start.19) | collective-permute-done | bytes 524320 | tf_op jit(solution)/shard_map/ppermute | solution.py:35
  102.6 0.3 collective-permute-start.39
  102.9 0.5 collective-permute-start.40
  103.5 1.6 %collective-permute-start.24 = (bf16[1024,256]{1,0:T(8,128)(2,1)S(1)}, bf16[1024,256]{1,0:T(8,128)(2,1)S(1)}, u32[]{:S(2)}, u32[]{:S(2)}) collective-permute-start(bf16[1024,256]{1,0:T(8,128)(2,1)S(1)} %collective-permute-done.23.refs_13_), channel_id=1, source_target_pairs={{0,1},{1,0},{2,3},{3,2},{4,5},{5,4},{6,7},{7,6},{8,9},{9,8},{10,11... | collective-permute-start | bytes 1572872 | tf_op jit(solution)/shard_map/ppermute | solution.py:39
  105.2 5.8 %collective-permute-done.39.refs_41_ = bf16[1024,256]{1,0:T(8,128)(2,1)S(1)} collective-permute-done((bf16[1024,256]{1,0:T(8,128)(2,1)S(1)}, bf16[1024,256]{1,0:T(8,128)(2,1)S(1)}, u32[]{:S(2)}, u32[]{:S(2)}) %collective-permute-start.39) | collective-permute-done | bytes 524320 | tf_op jit(solution)/shard_map/ppermute | solution.py:48
  111.2 5.4 %collective-permute-done.40.refs_42_ = bf16[1024,256]{1,0:T(8,128)(2,1)S(1)} collective-permute-done((bf16[1024,256]{1,0:T(8,128)(2,1)S(1)}, bf16[1024,256]{1,0:T(8,128)(2,1)S(1)}, u32[]{:S(2)}, u32[]{:S(2)}) %collective-permute-start.40) | collective-permute-done | bytes 524320 | tf_op jit(solution)/shard_map/ppermute | solution.py:48
  116.6 1.9 %collective-permute-start.21 = (bf16[1024,256]{1,0:T(8,128)(2,1)S(1)}, bf16[1024,256]{1,0:T(8,128)(2,1)}, u32[]{:S(2)}, u32[]{:S(2)}) collective-permute-start(bf16[1024,256]{1,0:T(8,128)(2,1)S(1)} %collective-permute-done.17.refs_9_.refs_18_), channel_id=1, source_target_pairs={{0,2},{1,3},{2,0},{3,1},{4,6},{5,7},{6,4},{7,5},{8,10},{9,11},{10,... | collective-permute-start | bytes 1572872 | tf_op jit(solution)/shard_map/ppermute | solution.py:35
  118.4 2.7 %collective-permute-start.18 = (bf16[1024,256]{1,0:T(8,128)(2,1)S(1)}, bf16[1024,256]{1,0:T(8,128)(2,1)S(1)}, u32[]{:S(2)}, u32[]{:S(2)}) collective-permute-start(bf16[1024,256]{1,0:T(8,128)(2,1)S(1)} %collective-permute-done.17.refs_9_.refs_18_), channel_id=1, source_target_pairs={{0,1},{1,0},{2,3},{3,2},{4,5},{5,4},{6,7},{7,6},{8,9},{9,8},{10,11... | collective-permute-start | bytes 1572872 | tf_op jit(solution)/shard_map/ppermute | solution.py:39
  121.2 2.9 %collective-permute-start.20 = (bf16[1024,256]{1,0:T(8,128)(2,1)}, bf16[1024,256]{1,0:T(8,128)(2,1)}, u32[]{:S(2)}, u32[]{:S(2)}) collective-permute-start(bf16[1024,256]{1,0:T(8,128)(2,1)} %collective-permute-done.19.refs_19_), channel_id=1, source_target_pairs={{0,1},{1,0},{2,3},{3,2},{4,5},{5,4},{6,7},{7,6},{8,9},{9,8},{10,11... | collective-permute-start | bytes 1572872 | tf_op jit(solution)/shard_map/ppermute | solution.py:39
  124.1 5.1 %collective-permute-done.21.refs_20_ = bf16[1024,256]{1,0:T(8,128)(2,1)} collective-permute-done((bf16[1024,256]{1,0:T(8,128)(2,1)S(1)}, bf16[1024,256]{1,0:T(8,128)(2,1)}, u32[]{:S(2)}, u32[]{:S(2)}) %collective-permute-start.21) | collective-permute-done | bytes 524320 | tf_op jit(solution)/shard_map/ppermute | solution.py:35
  129.2 3.3 %collective-permute-start.26 = (bf16[1024,256]{1,0:T(8,128)(2,1)}, bf16[1024,256]{1,0:T(8,128)(2,1)}, u32[]{:S(2)}, u32[]{:S(2)}) collective-permute-start(bf16[1024,256]{1,0:T(8,128)(2,1)} %collective-permute-done.25.refs_15_), channel_id=1, source_target_pairs={{0,1},{1,0},{2,3},{3,2},{4,5},{5,4},{6,7},{7,6},{8,9},{9,8},{10,11... | collective-permute-start | bytes 1572872 | tf_op jit(solution)/shard_map/ppermute | solution.py:39
  132.6 0.8 copy-done.24
  133.4 6.5 %shard_map.56.refs_43_ = f32[2,1024,256]{2,1,0:T(8,128)} custom-call(bf16[1024,256]{1,0:T(8,128)(2,1)} %copy-done, bf16[1024,256]{1,0:T(8,128)(2,1)} %copy-done.3, bf16[1024,256]{1,0:T(8,128)(2,1)} %copy-done.9, bf16[1024,256]{1,0:T(8,128)(2,1)} %copy-done.18, bf16[1024,256]{1,0:T(8,128)(2,1)} %copy-done.16, bf16[1024,256]{1,0:T(8,128)(2,1)} %copy-done.23, ...), custom_call_target="tpu_custom_call" | custom-call | flops 3758096384 | bytes 11010048 | tf_op jit(solution)/shard_map/pallas_call | solution.py:258
  140.0 10.0 %shard_map.57 = bf16[2,1024,256]{2,1,0:T(8,128)(2,1)} custom-call(bf16[1024,256]{1,0:T(8,128)(2,1)} %copy-done, bf16[1024,256]{1,0:T(8,128)(2,1)} %copy-done.3, bf16[2,1024,256]{2,1,0:T(8,128)(2,1)} %copy-done.1, bf16[1024,256]{1,0:T(8,128)(2,1)} %copy-done.9, bf16[1024,256]{1,0:T(8,128)(2,1)} %copy-done.18, ...), custom_call_target="tpu_custom_call" | custom-call | flops 5905580032 | bytes 17301504 | tf_op jit(solution)/shard_map/pallas_call | solution.py:258
  (106 shorter events, 1.4 us)
Async XLA Ops:
  2.2 131.1 %copy-start = (bf16[1024,256]{1,0:T(8,128)(2,1)}, bf16[1024,256]{1,0:T(8,128)(2,1)S(1)}, u32[]{:S(2)}) copy-start(bf16[1024,256]{1,0:T(8,128)(2,1)S(1)} %bitcast_multiply_fusion.refs_0_) | copy-start | bytes 1572868
  2.3 14.7 %collective-permute-start.3 = (bf16[1024,256]{1,0:T(8,128)(2,1)S(1)}, bf16[1024,256]{1,0:T(8,128)(2,1)S(1)}, u32[]{:S(2)}, u32[]{:S(2)}) collective-permute-start(bf16[1024,256]{1,0:T(8,128)(2,1)S(1)} %bitcast_multiply_fusion.refs_0_), channel_id=1, source_target_pairs={{0,4},{1,29},{2,6},{3,31},{4,8},{5,1},{6,10},{7,3},{8,12},{9,5},{1... | collective-permute-start | bytes 1572872 | tf_op jit(solution)/shard_map/ppermute | solution.py:31
  8.7 14.5 %collective-permute-start.1 = (bf16[1024,256]{1,0:T(8,128)(2,1)S(1)}, bf16[1024,256]{1,0:T(8,128)(2,1)S(1)}, u32[]{:S(2)}, u32[]{:S(2)}) collective-permute-start(bf16[1024,256]{1,0:T(8,128)(2,1)S(1)} %bitcast_multiply_fusion.refs_0_), channel_id=1, source_target_pairs={{0,2},{1,3},{2,0},{3,1},{4,6},{5,7},{6,4},{7,5},{8,10},{9,11},{10,... | collective-permute-start | bytes 1572872 | tf_op jit(solution)/shard_map/ppermute | solution.py:35
  11.5 13.9 %collective-permute-start = (bf16[1024,256]{1,0:T(8,128)(2,1)S(1)}, bf16[1024,256]{1,0:T(8,128)(2,1)S(1)}, u32[]{:S(2)}, u32[]{:S(2)}) collective-permute-start(bf16[1024,256]{1,0:T(8,128)(2,1)S(1)} %bitcast_multiply_fusion.refs_0_), channel_id=1, source_target_pairs={{0,1},{1,0},{2,3},{3,2},{4,5},{5,4},{6,7},{7,6},{8,9},{9,8},{10,11... | collective-permute-start | bytes 1572872 | tf_op jit(solution)/shard_map/ppermute | solution.py:39
  13.9 11.7 %collective-permute-start.29 = (bf16[1024,256]{1,0:T(8,128)(2,1)}, bf16[1024,256]{1,0:T(8,128)(2,1)S(1)}, u32[]{:S(2)}, u32[]{:S(2)}) collective-permute-start(bf16[1024,256]{1,0:T(8,128)(2,1)} %get-tuple-element.7.refs_14_.refs_27_), channel_id=1, source_target_pairs={{0,64},{1,193},{2,66},{3,195},{4,68},{5,197},{6,70},{7,199},{8,72}... | collective-permute-start | bytes 1572872 | tf_op jit(solution)/shard_map/ppermute | solution.py:48
  16.6 18.7 %collective-permute-start.27 = (bf16[1024,256]{1,0:T(8,128)(2,1)}, bf16[1024,256]{1,0:T(8,128)(2,1)S(1)}, u32[]{:S(2)}, u32[]{:S(2)}) collective-permute-start(bf16[1024,256]{1,0:T(8,128)(2,1)} %get-tuple-element.7.refs_14_.refs_27_), channel_id=1, source_target_pairs={{0,32},{32,0},{64,96},{96,64},{128,160},{160,128},{192,224},{224,1... | collective-permute-start | bytes 1572872 | tf_op jit(solution)/shard_map/ppermute | solution.py:52
  17.0 116.4 %copy-start.2 = (bf16[1024,256]{1,0:T(8,128)(2,1)}, bf16[1024,256]{1,0:T(8,128)(2,1)S(1)}, u32[]{:S(2)}) copy-start(bf16[1024,256]{1,0:T(8,128)(2,1)S(1)} %collective-permute-done.3.refs_12_.refs_24_) | copy-start | bytes 1572868
  17.0 18.4 %collective-permute-start.30 = (bf16[1024,256]{1,0:T(8,128)(2,1)}, bf16[1024,256]{1,0:T(8,128)(2,1)S(1)}, u32[]{:S(2)}, u32[]{:S(2)}) collective-permute-start(bf16[1024,256]{1,0:T(8,128)(2,1)} %get-tuple-element.8.refs_15_.refs_28_), channel_id=1, source_target_pairs={{0,64},{1,193},{2,66},{3,195},{4,68},{5,197},{6,70},{7,199},{8,72}... | collective-permute-start | bytes 1572872 | tf_op jit(solution)/shard_map/ppermute | solution.py:48
  23.2 21.0 %collective-permute-start.28 = (bf16[1024,256]{1,0:T(8,128)(2,1)}, bf16[1024,256]{1,0:T(8,128)(2,1)S(1)}, u32[]{:S(2)}, u32[]{:S(2)}) collective-permute-start(bf16[1024,256]{1,0:T(8,128)(2,1)} %get-tuple-element.8.refs_15_.refs_28_), channel_id=1, source_target_pairs={{0,32},{32,0},{64,96},{96,64},{128,160},{160,128},{192,224},{224,1... | collective-permute-start | bytes 1572872 | tf_op jit(solution)/shard_map/ppermute | solution.py:52
  25.4 108.0 %copy-start.3 = (bf16[1024,256]{1,0:T(8,128)(2,1)}, bf16[1024,256]{1,0:T(8,128)(2,1)S(1)}, u32[]{:S(2)}) copy-start(bf16[1024,256]{1,0:T(8,128)(2,1)S(1)} %collective-permute-done.refs_1_) | copy-start | bytes 1572868
  25.4 21.6 %collective-permute-start.9 = (bf16[1024,256]{1,0:T(8,128)(2,1)S(1)}, bf16[1024,256]{1,0:T(8,128)(2,1)S(1)}, u32[]{:S(2)}, u32[]{:S(2)}) collective-permute-start(bf16[1024,256]{1,0:T(8,128)(2,1)S(1)} %collective-permute-done.3.refs_12_.refs_24_), channel_id=1, source_target_pairs={{0,4},{1,29},{2,6},{3,31},{4,8},{5,1},{6,10},{7,3},{8,12},{9,5},{1... | collective-permute-start | bytes 1572872 | tf_op jit(solution)/shard_map/ppermute | solution.py:31
  25.6 107.8 %copy-start.4 = (bf16[1024,256]{1,0:T(8,128)(2,1)}, bf16[1024,256]{1,0:T(8,128)(2,1)S(1)}, u32[]{:S(2)}) copy-start(bf16[1024,256]{1,0:T(8,128)(2,1)S(1)} %collective-permute-done.29.refs_18_.refs_31_) | copy-start | bytes 1572868
  25.6 21.8 %collective-permute-start.4 = (bf16[1024,256]{1,0:T(8,128)(2,1)S(1)}, bf16[1024,256]{1,0:T(8,128)(2,1)S(1)}, u32[]{:S(2)}, u32[]{:S(2)}) collective-permute-start(bf16[1024,256]{1,0:T(8,128)(2,1)S(1)} %collective-permute-done.3.refs_12_.refs_24_), channel_id=1, source_target_pairs={{0,1},{1,0},{2,3},{3,2},{4,5},{5,4},{6,7},{7,6},{8,9},{9,8},{10,11... | collective-permute-start | bytes 1572872 | tf_op jit(solution)/shard_map/ppermute | solution.py:39
  35.3 98.0 %copy-start.5 = (bf16[1024,256]{1,0:T(8,128)(2,1)}, bf16[1024,256]{1,0:T(8,128)(2,1)S(1)}, u32[]{:S(2)}) copy-start(bf16[1024,256]{1,0:T(8,128)(2,1)S(1)} %collective-permute-done.27.refs_16_.refs_29_) | copy-start | bytes 1572868
  35.3 12.2 %collective-permute-start.2 = (bf16[1024,256]{1,0:T(8,128)(2,1)S(1)}, bf16[1024,256]{1,0:T(8,128)(2,1)S(1)}, u32[]{:S(2)}, u32[]{:S(2)}) collective-permute-start(bf16[1024,256]{1,0:T(8,128)(2,1)S(1)} %collective-permute-done.1), channel_id=1, source_target_pairs={{0,1},{1,0},{2,3},{3,2},{4,5},{5,4},{6,7},{7,6},{8,9},{9,8},{10,11... | collective-permute-start | bytes 1572872 | tf_op jit(solution)/shard_map/ppermute | solution.py:39
  35.4 12.4 %collective-permute-start.5 = (bf16[1024,256]{1,0:T(8,128)(2,1)S(1)}, bf16[1024,256]{1,0:T(8,128)(2,1)S(1)}, u32[]{:S(2)}, u32[]{:S(2)}) collective-permute-start(bf16[1024,256]{1,0:T(8,128)(2,1)S(1)} %collective-permute-done.refs_1_), channel_id=1, source_target_pairs={{0,4},{1,29},{2,6},{3,31},{4,8},{5,1},{6,10},{7,3},{8,12},{9,5},{1... | collective-permute-start | bytes 1572872 | tf_op jit(solution)/shard_map/ppermute | solution.py:31
  44.2 52.7 %copy-start.7 = (bf16[1024,256]{1,0:T(8,128)(2,1)}, bf16[1024,256]{1,0:T(8,128)(2,1)S(1)}, u32[]{:S(2)}) copy-start(bf16[1024,256]{1,0:T(8,128)(2,1)S(1)} %collective-permute-done.28.refs_17_.refs_30_) | copy-start | bytes 1572868
  44.2 8.9 %collective-permute-start.33 = (bf16[1024,256]{1,0:T(8,128)(2,1)S(1)}, bf16[1024,256]{1,0:T(8,128)(2,1)S(1)}, u32[]{:S(2)}, u32[]{:S(2)}) collective-permute-start(bf16[1024,256]{1,0:T(8,128)(2,1)S(1)} %collective-permute-done.29.refs_18_.refs_31_), channel_id=1, source_target_pairs={{0,64},{1,193},{2,66},{3,195},{4,68},{5,197},{6,70},{7,199},{8,72}... | collective-permute-start | bytes 1572872 | tf_op jit(solution)/shard_map/ppermute | solution.py:48
  47.0 11.7 %collective-permute-start.31 = (bf16[1024,256]{1,0:T(8,128)(2,1)S(1)}, bf16[1024,256]{1,0:T(8,128)(2,1)S(1)}, u32[]{:S(2)}, u32[]{:S(2)}) collective-permute-start(bf16[1024,256]{1,0:T(8,128)(2,1)S(1)} %collective-permute-done.27.refs_16_.refs_29_), channel_id=1, source_target_pairs={{0,64},{1,193},{2,66},{3,195},{4,68},{5,197},{6,70},{7,199},{8,72}... | collective-permute-start | bytes 1572872 | tf_op jit(solution)/shard_map/ppermute | solution.py:48
  47.4 16.9 %collective-permute-start.34 = (bf16[1024,256]{1,0:T(8,128)(2,1)S(1)}, bf16[1024,256]{1,0:T(8,128)(2,1)S(1)}, u32[]{:S(2)}, u32[]{:S(2)}) collective-permute-start(bf16[1024,256]{1,0:T(8,128)(2,1)S(1)} %collective-permute-done.30.refs_19_.refs_32_), channel_id=1, source_target_pairs={{0,64},{1,193},{2,66},{3,195},{4,68},{5,197},{6,70},{7,199},{8,72}... | collective-permute-start | bytes 1572872 | tf_op jit(solution)/shard_map/ppermute | solution.py:48
  47.6 22.3 %collective-permute-start.32 = (bf16[1024,256]{1,0:T(8,128)(2,1)S(1)}, bf16[1024,256]{1,0:T(8,128)(2,1)S(1)}, u32[]{:S(2)}, u32[]{:S(2)}) collective-permute-start(bf16[1024,256]{1,0:T(8,128)(2,1)S(1)} %collective-permute-done.28.refs_17_.refs_30_), channel_id=1, source_target_pairs={{0,64},{1,193},{2,66},{3,195},{4,68},{5,197},{6,70},{7,199},{8,72}... | collective-permute-start | bytes 1572872 | tf_op jit(solution)/shard_map/ppermute | solution.py:48
  47.8 24.9 %collective-permute-start.15 = (bf16[1024,256]{1,0:T(8,128)(2,1)S(1)}, bf16[1024,256]{1,0:T(8,128)(2,1)S(1)}, u32[]{:S(2)}, u32[]{:S(2)}) collective-permute-start(bf16[1024,256]{1,0:T(8,128)(2,1)S(1)} %collective-permute-done.9.refs_10_.refs_21_), channel_id=1, source_target_pairs={{0,4},{1,29},{2,6},{3,31},{4,8},{5,1},{6,10},{7,3},{8,12},{9,5},{1... | collective-permute-start | bytes 1572872 | tf_op jit(solution)/shard_map/ppermute | solution.py:31
  53.1 22.7 %collective-permute-start.10 = (bf16[1024,256]{1,0:T(8,128)(2,1)S(1)}, bf16[1024,256]{1,0:T(8,128)(2,1)S(1)}, u32[]{:S(2)}, u32[]{:S(2)}) collective-permute-start(bf16[1024,256]{1,0:T(8,128)(2,1)S(1)} %collective-permute-done.9.refs_10_.refs_21_), channel_id=1, source_target_pairs={{0,1},{1,0},{2,3},{3,2},{4,5},{5,4},{6,7},{7,6},{8,9},{9,8},{10,11... | collective-permute-start | bytes 1572872 | tf_op jit(solution)/shard_map/ppermute | solution.py:39
  58.7 17.2 %collective-permute-start.11 = (bf16[1024,256]{1,0:T(8,128)(2,1)S(1)}, bf16[1024,256]{1,0:T(8,128)(2,1)S(1)}, u32[]{:S(2)}, u32[]{:S(2)}) collective-permute-start(bf16[1024,256]{1,0:T(8,128)(2,1)S(1)} %collective-permute-done.5.refs_13_.refs_25_), channel_id=1, source_target_pairs={{0,4},{1,29},{2,6},{3,31},{4,8},{5,1},{6,10},{7,3},{8,12},{9,5},{1... | collective-permute-start | bytes 1572872 | tf_op jit(solution)/shard_map/ppermute | solution.py:31
  64.3 11.7 %collective-permute-start.6 = (bf16[1024,256]{1,0:T(8,128)(2,1)S(1)}, bf16[1024,256]{1,0:T(8,128)(2,1)S(1)}, u32[]{:S(2)}, u32[]{:S(2)}) collective-permute-start(bf16[1024,256]{1,0:T(8,128)(2,1)S(1)} %collective-permute-done.5.refs_13_.refs_25_), channel_id=1, source_target_pairs={{0,1},{1,0},{2,3},{3,2},{4,5},{5,4},{6,7},{7,6},{8,9},{9,8},{10,11... | collective-permute-start | bytes 1572872 | tf_op jit(solution)/shard_map/ppermute | solution.py:39
  65.7 74.3 %copy-start.1 = (bf16[2,1024,256]{2,1,0:T(8,128)(2,1)}, bf16[2,1024,256]{2,1,0:T(8,128)(2,1)S(1)}, u32[]{:S(2)}) copy-start(bf16[2,1024,256]{2,1,0:T(8,128)(2,1)S(1)} %pad_maximum_fusion.refs_2_) | copy-start | bytes 3145732
  69.9 27.0 %collective-permute-start.7 = (bf16[2,1024,256]{2,1,0:T(8,128)(2,1)S(1)}, bf16[2,1024,256]{2,1,0:T(8,128)(2,1)}, u32[]{:S(2)}, u32[]{:S(2)}) collective-permute-start(bf16[2,1024,256]{2,1,0:T(8,128)(2,1)S(1)} %pad_maximum_fusion.refs_2_), channel_id=1, source_target_pairs={{0,4},{1,29},{2,6},{3,31},{4,8},{5,1},{6,10},{7,3},{8,12},{9,5},{1... | collective-permute-start | bytes 3145736 | tf_op jit(solution)/shard_map/ppermute | solution.py:31
  72.7 9.2 %collective-permute-start.37 = (bf16[1024,256]{1,0:T(8,128)(2,1)S(1)}, bf16[1024,256]{1,0:T(8,128)(2,1)S(1)}, u32[]{:S(2)}, u32[]{:S(2)}) collective-permute-start(bf16[1024,256]{1,0:T(8,128)(2,1)S(1)} %collective-permute-done.33.refs_22_.refs_35_), channel_id=1, source_target_pairs={{0,64},{1,193},{2,66},{3,195},{4,68},{5,197},{6,70},{7,199},{8,72}... | collective-permute-start | bytes 1572872 | tf_op jit(solution)/shard_map/ppermute | solution.py:48
  75.8 11.7 %collective-permute-start.35 = (bf16[1024,256]{1,0:T(8,128)(2,1)S(1)}, bf16[1024,256]{1,0:T(8,128)(2,1)S(1)}, u32[]{:S(2)}, u32[]{:S(2)}) collective-permute-start(bf16[1024,256]{1,0:T(8,128)(2,1)S(1)} %collective-permute-done.31.refs_20_.refs_33_), channel_id=1, source_target_pairs={{0,64},{1,193},{2,66},{3,195},{4,68},{5,197},{6,70},{7,199},{8,72}... | collective-permute-start | bytes 1572872 | tf_op jit(solution)/shard_map/ppermute | solution.py:48
  75.9 17.3 %collective-permute-start.38 = (bf16[1024,256]{1,0:T(8,128)(2,1)S(1)}, bf16[1024,256]{1,0:T(8,128)(2,1)S(1)}, u32[]{:S(2)}, u32[]{:S(2)}) collective-permute-start(bf16[1024,256]{1,0:T(8,128)(2,1)S(1)} %collective-permute-done.34.refs_23_.refs_36_), channel_id=1, source_target_pairs={{0,64},{1,193},{2,66},{3,195},{4,68},{5,197},{6,70},{7,199},{8,72}... | collective-permute-start | bytes 1572872 | tf_op jit(solution)/shard_map/ppermute | solution.py:48
  76.0 17.9 %collective-permute-start.36 = (bf16[1024,256]{1,0:T(8,128)(2,1)S(1)}, bf16[1024,256]{1,0:T(8,128)(2,1)S(1)}, u32[]{:S(2)}, u32[]{:S(2)}) collective-permute-start(bf16[1024,256]{1,0:T(8,128)(2,1)S(1)} %collective-permute-done.34.refs_23_.refs_36_), channel_id=1, source_target_pairs={{0,32},{32,0},{64,96},{96,64},{128,160},{160,128},{192,224},{224,1... | collective-permute-start | bytes 1572872 | tf_op jit(solution)/shard_map/ppermute | solution.py:52
  81.9 16.7 %collective-permute-start.23 = (bf16[1024,256]{1,0:T(8,128)(2,1)S(1)}, bf16[1024,256]{1,0:T(8,128)(2,1)S(1)}, u32[]{:S(2)}, u32[]{:S(2)}) collective-permute-start(bf16[1024,256]{1,0:T(8,128)(2,1)S(1)} %collective-permute-done.15.refs_8_.refs_17_), channel_id=1, source_target_pairs={{0,4},{1,29},{2,6},{3,31},{4,8},{5,1},{6,10},{7,3},{8,12},{9,5},{1... | collective-permute-start | bytes 1572872 | tf_op jit(solution)/shard_map/ppermute | solution.py:31
  87.5 15.1 %collective-permute-start.19 = (bf16[1024,256]{1,0:T(8,128)(2,1)S(1)}, bf16[1024,256]{1,0:T(8,128)(2,1)}, u32[]{:S(2)}, u32[]{:S(2)}) collective-permute-start(bf16[1024,256]{1,0:T(8,128)(2,1)S(1)} %collective-permute-done.15.refs_8_.refs_17_), channel_id=1, source_target_pairs={{0,2},{1,3},{2,0},{3,1},{4,6},{5,7},{6,4},{7,5},{8,10},{9,11},{10,... | collective-permute-start | bytes 1572872 | tf_op jit(solution)/shard_map/ppermute | solution.py:35
  93.2 9.7 %collective-permute-start.16 = (bf16[1024,256]{1,0:T(8,128)(2,1)S(1)}, bf16[1024,256]{1,0:T(8,128)(2,1)S(1)}, u32[]{:S(2)}, u32[]{:S(2)}) collective-permute-start(bf16[1024,256]{1,0:T(8,128)(2,1)S(1)} %collective-permute-done.15.refs_8_.refs_17_), channel_id=1, source_target_pairs={{0,1},{1,0},{2,3},{3,2},{4,5},{5,4},{6,7},{7,6},{8,9},{9,8},{10,11... | collective-permute-start | bytes 1572872 | tf_op jit(solution)/shard_map/ppermute | solution.py:39
  93.9 9.5 %collective-permute-start.17 = (bf16[1024,256]{1,0:T(8,128)(2,1)S(1)}, bf16[1024,256]{1,0:T(8,128)(2,1)S(1)}, u32[]{:S(2)}, u32[]{:S(2)}) collective-permute-start(bf16[1024,256]{1,0:T(8,128)(2,1)S(1)} %collective-permute-done.11.refs_11_.refs_22_), channel_id=1, source_target_pairs={{0,4},{1,29},{2,6},{3,31},{4,8},{5,1},{6,10},{7,3},{8,12},{9,5},{1... | collective-permute-start | bytes 1572872 | tf_op jit(solution)/shard_map/ppermute | solution.py:31
  96.9 24.2 %collective-permute-start.13 = (bf16[2,1024,256]{2,1,0:T(8,128)(2,1)}, bf16[2,1024,256]{2,1,0:T(8,128)(2,1)}, u32[]{:S(2)}, u32[]{:S(2)}) collective-permute-start(bf16[2,1024,256]{2,1,0:T(8,128)(2,1)} %collective-permute-done.7.refs_26_), channel_id=1, source_target_pairs={{0,4},{1,29},{2,6},{3,31},{4,8},{5,1},{6,10},{7,3},{8,12},{9,5},{1... | collective-permute-start | bytes 3145736 | tf_op jit(solution)/shard_map/ppermute | solution.py:31
  98.6 6.5 %collective-permute-start.12 = (bf16[1024,256]{1,0:T(8,128)(2,1)S(1)}, bf16[1024,256]{1,0:T(8,128)(2,1)S(1)}, u32[]{:S(2)}, u32[]{:S(2)}) collective-permute-start(bf16[1024,256]{1,0:T(8,128)(2,1)S(1)} %collective-permute-done.11.refs_11_.refs_22_), channel_id=1, source_target_pairs={{0,1},{1,0},{2,3},{3,2},{4,5},{5,4},{6,7},{7,6},{8,9},{9,8},{10,11... | collective-permute-start | bytes 1572872 | tf_op jit(solution)/shard_map/ppermute | solution.py:39
  102.6 8.4 %collective-permute-start.39 = (bf16[1024,256]{1,0:T(8,128)(2,1)S(1)}, bf16[1024,256]{1,0:T(8,128)(2,1)S(1)}, u32[]{:S(2)}, u32[]{:S(2)}) collective-permute-start(bf16[1024,256]{1,0:T(8,128)(2,1)S(1)} %collective-permute-done.35.refs_24_.refs_37_), channel_id=1, source_target_pairs={{0,64},{1,193},{2,66},{3,195},{4,68},{5,197},{6,70},{7,199},{8,72}... | collective-permute-start | bytes 1572872 | tf_op jit(solution)/shard_map/ppermute | solution.py:48
  102.9 13.7 %collective-permute-start.40 = (bf16[1024,256]{1,0:T(8,128)(2,1)S(1)}, bf16[1024,256]{1,0:T(8,128)(2,1)S(1)}, u32[]{:S(2)}, u32[]{:S(2)}) collective-permute-start(bf16[1024,256]{1,0:T(8,128)(2,1)S(1)} %collective-permute-done.36.refs_25_.refs_38_), channel_id=1, source_target_pairs={{0,64},{1,193},{2,66},{3,195},{4,68},{5,197},{6,70},{7,199},{8,72}... | collective-permute-start | bytes 1572872 | tf_op jit(solution)/shard_map/ppermute | solution.py:48
  103.5 15.0 %collective-permute-start.24 = (bf16[1024,256]{1,0:T(8,128)(2,1)S(1)}, bf16[1024,256]{1,0:T(8,128)(2,1)S(1)}, u32[]{:S(2)}, u32[]{:S(2)}) collective-permute-start(bf16[1024,256]{1,0:T(8,128)(2,1)S(1)} %collective-permute-done.23.refs_13_), channel_id=1, source_target_pairs={{0,1},{1,0},{2,3},{3,2},{4,5},{5,4},{6,7},{7,6},{8,9},{9,8},{10,11... | collective-permute-start | bytes 1572872 | tf_op jit(solution)/shard_map/ppermute | solution.py:39
  105.1 34.9 %collective-permute-start.8 = (bf16[2,1024,256]{2,1,0:T(8,128)(2,1)}, bf16[2,1024,256]{2,1,0:T(8,128)(2,1)}, u32[]{:S(2)}, u32[]{:S(2)}) collective-permute-start(bf16[2,1024,256]{2,1,0:T(8,128)(2,1)} %collective-permute-done.7.refs_26_), channel_id=1, source_target_pairs={{0,1},{1,0},{2,3},{3,2},{4,5},{5,4},{6,7},{7,6},{8,9},{9,8},{10,11... | collective-permute-start | bytes 3145736 | tf_op jit(solution)/shard_map/ppermute | solution.py:39
  111.0 10.2 %collective-permute-start.25 = (bf16[1024,256]{1,0:T(8,128)(2,1)}, bf16[1024,256]{1,0:T(8,128)(2,1)}, u32[]{:S(2)}, u32[]{:S(2)}) collective-permute-start(bf16[1024,256]{1,0:T(8,128)(2,1)} %collective-permute-done.19.refs_19_), channel_id=1, source_target_pairs={{0,4},{1,29},{2,6},{3,31},{4,8},{5,1},{6,10},{7,3},{8,12},{9,5},{1... | collective-permute-start | bytes 1572872 | tf_op jit(solution)/shard_map/ppermute | solution.py:31
  116.6 12.6 %collective-permute-start.21 = (bf16[1024,256]{1,0:T(8,128)(2,1)S(1)}, bf16[1024,256]{1,0:T(8,128)(2,1)}, u32[]{:S(2)}, u32[]{:S(2)}) collective-permute-start(bf16[1024,256]{1,0:T(8,128)(2,1)S(1)} %collective-permute-done.17.refs_9_.refs_18_), channel_id=1, source_target_pairs={{0,2},{1,3},{2,0},{3,1},{4,6},{5,7},{6,4},{7,5},{8,10},{9,11},{10,... | collective-permute-start | bytes 1572872 | tf_op jit(solution)/shard_map/ppermute | solution.py:35
  118.4 14.1 %collective-permute-start.18 = (bf16[1024,256]{1,0:T(8,128)(2,1)S(1)}, bf16[1024,256]{1,0:T(8,128)(2,1)S(1)}, u32[]{:S(2)}, u32[]{:S(2)}) collective-permute-start(bf16[1024,256]{1,0:T(8,128)(2,1)S(1)} %collective-permute-done.17.refs_9_.refs_18_), channel_id=1, source_target_pairs={{0,1},{1,0},{2,3},{3,2},{4,5},{5,4},{6,7},{7,6},{8,9},{9,8},{10,11... | collective-permute-start | bytes 1572872 | tf_op jit(solution)/shard_map/ppermute | solution.py:39
  121.1 18.9 %collective-permute-start.14 = (bf16[2,1024,256]{2,1,0:T(8,128)(2,1)}, bf16[2,1024,256]{2,1,0:T(8,128)(2,1)}, u32[]{:S(2)}, u32[]{:S(2)}) collective-permute-start(bf16[2,1024,256]{2,1,0:T(8,128)(2,1)} %collective-permute-done.13.refs_23_), channel_id=1, source_target_pairs={{0,1},{1,0},{2,3},{3,2},{4,5},{5,4},{6,7},{7,6},{8,9},{9,8},{10,11... | collective-permute-start | bytes 3145736 | tf_op jit(solution)/shard_map/ppermute | solution.py:39
  121.2 18.7 %collective-permute-start.20 = (bf16[1024,256]{1,0:T(8,128)(2,1)}, bf16[1024,256]{1,0:T(8,128)(2,1)}, u32[]{:S(2)}, u32[]{:S(2)}) collective-permute-start(bf16[1024,256]{1,0:T(8,128)(2,1)} %collective-permute-done.19.refs_19_), channel_id=1, source_target_pairs={{0,1},{1,0},{2,3},{3,2},{4,5},{5,4},{6,7},{7,6},{8,9},{9,8},{10,11... | collective-permute-start | bytes 1572872 | tf_op jit(solution)/shard_map/ppermute | solution.py:39
  129.2 10.8 %collective-permute-start.26 = (bf16[1024,256]{1,0:T(8,128)(2,1)}, bf16[1024,256]{1,0:T(8,128)(2,1)}, u32[]{:S(2)}, u32[]{:S(2)}) collective-permute-start(bf16[1024,256]{1,0:T(8,128)(2,1)} %collective-permute-done.25.refs_15_), channel_id=1, source_target_pairs={{0,1},{1,0},{2,3},{3,2},{4,5},{5,4},{6,7},{7,6},{8,9},{9,8},{10,11... | collective-permute-start | bytes 1572872 | tf_op jit(solution)/shard_map/ppermute | solution.py:39
  133.4 6.6 %collective-permute-start.22 = (bf16[1024,256]{1,0:T(8,128)(2,1)}, bf16[1024,256]{1,0:T(8,128)(2,1)}, u32[]{:S(2)}, u32[]{:S(2)}) collective-permute-start(bf16[1024,256]{1,0:T(8,128)(2,1)} %collective-permute-done.21.refs_20_), channel_id=1, source_target_pairs={{0,1},{1,0},{2,3},{3,2},{4,5},{5,4},{6,7},{7,6},{8,9},{9,8},{10,11... | collective-permute-start | bytes 1572872 | tf_op jit(solution)/shard_map/ppermute | solution.py:39
  (25 other events, 652.4 us)
